TPU v7x, 8 devices: a whole 2x2x1 slice. The times are simulated.
8 devices in a mesh: dp: 1 (over z), tp: 2 (over y), role: 4 (over x, core).
Axes of the slice: x: 2, y: 2, z: 1, core: 2. Of those that a mesh axis runs over, the one named last changes fastest.
Arguments:
- hidden: bfloat16 [2, 64, 2048], P(None, 'dp')
- segment_ids: int32 [64], P('dp')
- loss_mask: int32 [64], P('dp')
- target: int32 [64], P('dp')
- norm_gains: float32 [2, 3, 2048], replicated
- w_query: bfloat16 [4096, 2048], P(('role', 'tp'))
- b_query: bfloat16 [64, 64], P(('role', 'tp'))
- w_key: bfloat16 [512, 2048], P('role')
- b_key: bfloat16 [8, 64], P('role')
- w_value: bfloat16 [512, 2048], P('role')
- b_value: bfloat16 [8, 64], P('role')
- w_out: bfloat16 [4096, 2048], P(('role', 'tp'))
- w_gate: bfloat16 [11264, 2048], P(('role', 'tp'))
- w_up: bfloat16 [11264, 2048], P(('role', 'tp'))
- w_down: bfloat16 [11264, 2048], P(('role', 'tp'))
- w_head: bfloat16 [64000, 2048], P(('role', 'tp'))
Outputs:
- output 1: float32 [64], P('dp')
- output 2: float32 [64], P('dp')
All inputs are finite; a program needn't handle non-finite values.
Results may differ from a plain program's by a relative error of at most 0.00370071.
Values sent between devices are 32-bit elements.
A program may use at most 1 GiB of HBM per device.

v0:
```python
import functools
import jax
import jax.numpy as jnp
from jax import lax
from jax.sharding import PartitionSpec as P

EPS = 1e-6
ROPE_BASE = 1000000.0
value_a11 = 0.7
MODEL_AXES = ("tp", "role")


def rms_norm(values, gain):
    vals_f32 = values.astype(jnp.float32)
    inv_rms = lax.rsqrt(jnp.mean(vals_f32 * vals_f32, axis=-1, keepdims=True) + EPS)
    return (vals_f32 * inv_rms * gain).astype(jnp.bfloat16)


def segment_positions(segment_ids):
    tok_index = jnp.arange(segment_ids.shape[-1])
    prev_ids = jnp.concatenate([segment_ids[..., :1] - 1, segment_ids[..., :-1]], axis=-1)
    seg_start = lax.cummax(jnp.where(segment_ids != prev_ids, tok_index, 0), axis=segment_ids.ndim - 1)
    return tok_index - seg_start


def rotary(values, positions):
    half_dim = values.shape[-1] // 2
    inv_freq = ROPE_BASE ** (-2.0 * jnp.arange(half_dim).astype(jnp.float32) / values.shape[-1])
    angles = positions.astype(jnp.float32)[..., None] * inv_freq
    cos_part = jnp.cos(angles)[..., None, :]
    sin_part = jnp.sin(angles)[..., None, :]
    first_half = values[..., :half_dim]
    second_half = values[..., half_dim:]
    return jnp.concatenate([first_half * cos_part - second_half * sin_part, second_half * cos_part + first_half * sin_part], axis=-1)


def half_sum(partial_vals, half_idx):
    slot_pick = (jnp.arange(2) == half_idx).astype(partial_vals.dtype).reshape((2,) + (1,) * partial_vals.ndim)
    reduced = lax.psum(slot_pick * partial_vals[None], MODEL_AXES)
    return lax.dynamic_index_in_dim(reduced, half_idx, 0, keepdims=False)


def half_max(partial_vals, half_idx):
    slot_pick = (jnp.arange(2) == half_idx).reshape((2,) + (1,) * partial_vals.ndim)
    reduced = lax.pmax(jnp.where(slot_pick, partial_vals[None], -jnp.inf), MODEL_AXES)
    return lax.dynamic_index_in_dim(reduced, half_idx, 0, keepdims=False)


def last_layer(x_in, positions, allowed, gain3, w_query, b_query, w_key, b_key, w_value, b_value, w_out, w_gate, w_up, w_down, reduce_sum):
    tokens = x_in.shape[0]
    head_dim = b_query.shape[1]
    q_heads = b_query.shape[0]
    kv_heads = b_key.shape[0]
    normed = rms_norm(x_in, gain3[0])
    q_proj = jnp.einsum("td,kd->tk", normed, w_query, preferred_element_type=jnp.float32).reshape(tokens, q_heads, head_dim) + b_query.astype(jnp.float32)
    k_proj = jnp.einsum("td,kd->tk", normed, w_key, preferred_element_type=jnp.float32).reshape(tokens, kv_heads, head_dim) + b_key.astype(jnp.float32)
    v_proj = (jnp.einsum("td,kd->tk", normed, w_value, preferred_element_type=jnp.float32).reshape(tokens, kv_heads, head_dim) + b_value.astype(jnp.float32)).astype(jnp.bfloat16)
    q_rot = rotary(q_proj, positions).astype(jnp.bfloat16).reshape(tokens, kv_heads, q_heads // kv_heads, head_dim)
    k_rot = rotary(k_proj, positions).astype(jnp.bfloat16)
    scores = jnp.einsum("tkgd,skd->kgts", q_rot, k_rot, preferred_element_type=jnp.float32) * head_dim ** -0.5
    attn_probs = jax.nn.softmax(jnp.where(allowed, scores, -1e30), axis=-1).astype(jnp.bfloat16)
    attn = jnp.einsum("kgts,skd->tkgd", attn_probs, v_proj, preferred_element_type=jnp.float32).astype(jnp.bfloat16).reshape(tokens, q_heads * head_dim)
    resid = (x_in.astype(jnp.float32) + reduce_sum(jnp.dot(attn, w_out, preferred_element_type=jnp.float32))).astype(jnp.bfloat16)
    normed_mlp = rms_norm(resid, gain3[1])
    gate_proj = jnp.einsum("td,fd->tf", normed_mlp, w_gate, preferred_element_type=jnp.float32)
    up_proj = jnp.einsum("td,fd->tf", normed_mlp, w_up, preferred_element_type=jnp.float32)
    act_vals = (jax.nn.silu(gate_proj) * up_proj).astype(jnp.bfloat16)
    layer_out = (resid.astype(jnp.float32) + reduce_sum(jnp.dot(act_vals, w_down, preferred_element_type=jnp.float32))).astype(jnp.bfloat16)
    return rms_norm(layer_out, gain3[2])


def solution(mesh):
    tp_size = mesh.shape["tp"]
    half_roles = mesh.shape["role"] // 2
    shards = tp_size * half_roles
    back_pairs = [(half_roles + local_idx, local_idx) for local_idx in range(half_roles)]
    by_shard = P(("role", "tp"), None)
    by_role = P("role", None)

    def per_device(hidden, segment_ids, loss_mask, target, norm_gains, w_query, b_query, w_key, b_key, w_value, b_value, w_out, w_gate, w_up, w_down, w_head):
        role_index = lax.axis_index("role")
        half_idx = role_index // half_roles
        local_role = role_index % half_roles
        shard_idx = local_role * tp_size + lax.axis_index("tp")
        head_dim = b_query.shape[1]
        q_heads = b_query.shape[0]
        kv_role = b_key.shape[0]
        q_per_kv = (q_heads * shards) // (kv_role * half_roles)
        kv_need = max(q_heads // q_per_kv, 1)
        kv_first = (shard_idx * q_heads) // q_per_kv - local_role * kv_role
        tokens = segment_ids.shape[0]
        tok_index = jnp.arange(tokens)
        allowed = (segment_ids[:, None] == segment_ids[None, :]) & (tok_index[:, None] >= tok_index[None, :])
        final_rows = last_layer(
            lax.dynamic_index_in_dim(hidden, half_idx, 0, keepdims=False),
            segment_positions(segment_ids), allowed,
            lax.dynamic_index_in_dim(norm_gains, half_idx, 0, keepdims=False),
            w_query, b_query,
            lax.dynamic_slice_in_dim(w_key, kv_first * head_dim, kv_need * head_dim, axis=0),
            lax.dynamic_slice_in_dim(b_key, kv_first, kv_need, axis=0),
            lax.dynamic_slice_in_dim(w_value, kv_first * head_dim, kv_need * head_dim, axis=0),
            lax.dynamic_slice_in_dim(b_value, kv_first, kv_need, axis=0),
            w_out, w_gate, w_up, w_down, functools.partial(half_sum, half_idx=half_idx))
        logits = jnp.einsum("td,vd->tv", final_rows, w_head, preferred_element_type=jnp.float32) / value_a11
        row_max = half_max(jnp.max(logits, axis=-1), half_idx)
        sum_exp = half_sum(jnp.sum(jnp.exp(logits - row_max[:, None]), axis=-1), half_idx)
        log_probs = logits - (row_max + jnp.log(sum_exp))[:, None]
        ref_log_probs = lax.ppermute(log_probs, "role", back_pairs)
        kl_local = jnp.sum(jnp.exp(log_probs) * (log_probs - ref_log_probs), axis=-1)
        vocab_local = w_head.shape[0]
        vocab_ids = shard_idx * vocab_local + jnp.arange(vocab_local)
        tgt_local = jnp.sum(jnp.where(vocab_ids[None, :] == target[:, None], log_probs, 0.0), axis=-1)
        on_policy = (half_idx == 0).astype(jnp.float32)
        pair_sums = lax.psum(jnp.stack([kl_local, tgt_local]) * on_policy, MODEL_AXES)
        mask_vals = loss_mask.astype(jnp.float32)
        return pair_sums[0] * mask_vals, pair_sums[1] * mask_vals

    in_specs = (P(None, "dp", None), P("dp"), P("dp"), P("dp"), P(None, None, None), by_shard, by_shard, by_role, by_role, by_role, by_role, by_shard, by_shard, by_shard, by_shard, by_shard)
    return jax.shard_map(per_device, mesh=mesh, in_specs=in_specs, out_specs=(P("dp"), P("dp")), check_vma=False)
```

profile of v0, /device:TPU:0, one launch (start us, length us, event | category | flops | bytes accessed | tf_op | source)
XLA Modules:
  0.0 272.3 jit_solution(16586987517551770382)
XLA Ops:
  7.2 0.0 copy-start
  7.2 0.0 all-reduce.3.cloned.1.call-start
  7.3 1.2 fusion.13
  8.6 0.7 convert_element_type.115
  9.3 0.8 fusion.53
  10.7 0.8 fusion.71
  11.5 0.1 copy.22
  11.6 0.1 reduce-window.8
  11.7 0.1 reduce.2
  11.8 0.1 multiply_cosine_fusion
  12.0 0.8 constant_dynamic-slice_fusion.6
  12.8 0.7 fusion.73
  13.5 1.4 fusion.3
  14.9 0.1 fusion.66
  15.0 1.7 convolution_add_fusion
  16.8 0.0 copy-start.3
  16.8 0.2 fusion.85
  17.1 0.1 fusion.38
  17.1 1.6 convolution_convert_fusion
  18.7 0.0 copy-done.3
  18.7 0.5 fusion.87
  19.2 1.2 broadcast_multiply_fusion.1
  20.4 0.0 all-reduce.3.cloned.1.call-update
  20.5 0.0 all-reduce.5.cloned.1.call-start
  20.5 48.1 %all-reduce.3.cloned.1.call-done = f32[2,64,2048]{2,1,0:T(8,128)} async-done(((f32[2,64,2048]{2,1,0:T(8,128)}), f32[2,64,2048]{2,1,0:T(8,128)}) %all-reduce.3.cloned.1.call-update) | async-done | bytes 1048592 | tf_op jit(solution)/shard_map/psum | solution.py:39
  68.7 1.2 fusion.19
  69.9 4.5 %fusion.48 = f32[64,1408]{1,0:T(8,128)S(1)} fusion(bf16[1408,2048]{1,0:T(8,128)(2,1)} %param.28, bf16[64,2048]{1,0:T(8,128)(2,1)S(1)} %get-tuple-element.7, f32[2048]{0:T(1024)S(1)} %bitcast.101, f32[64]{0:T(128)S(1)} %add_rsqrt_fusion.1), kind=kOutput, calls=%fused_computation.67 | convolution fusion | flops 369623040 | bytes 6398208 | tf_op jit(solution)/shard_map/td,fd->tf/dot_general | solution.py:65
  74.4 7.4 %fusion.6 = f32[64,2048]{1,0:T(8,128)S(1)} fusion(bf16[1408,2048]{1,0:T(8,128)(2,1)} %param.30, bf16[1408,2048]{1,0:T(8,128)(2,1)} %param.29, f32[64,1408]{1,0:T(8,128)S(1)} %fusion.48, bf16[64,2048]{1,0:T(8,128)(2,1)S(1)} %get-tuple-element.7, f32[2048]{0:T(1024)S(1)} %bitcast.102, f32[64]{0:T(128)S(1)} %add_rsqrt_fusion.1), kind=kOutput, calls=%fused_computation.16 | convolution fusion | flops 739262464 | bytes 12689664 | tf_op jit(solution)/shard_map/dot_general | solution.py:68
  81.9 1.2 broadcast_multiply_fusion
  83.1 0.0 all-reduce.5.cloned.1.call-update
  83.1 44.7 %all-reduce.5.cloned.1.call-done = f32[2,64,2048]{2,1,0:T(8,128)} async-done(((f32[2,64,2048]{2,1,0:T(8,128)}), f32[2,64,2048]{2,1,0:T(8,128)}) %all-reduce.5.cloned.1.call-update) | async-done | bytes 1048592 | tf_op jit(solution)/shard_map/psum | solution.py:39
  127.8 1.2 fusion.10
  129.0 15.3 %fusion.86 = (f32[64]{0:T(128)S(1)}, f32[64,8000]{1,0:T(8,128)S(1)}) fusion(bf16[8000,2048]{1,0:T(8,128)(2,1)} %param.31, bf16[64,2048]{1,0:T(8,128)(2,1)S(1)} %get-tuple-element.5, f32[2048]{0:T(1024)S(1)} %bitcast.99, f32[64]{0:T(128)S(1)} %add_rsqrt_fusion), kind=kOutput, calls=%fused_computation.124 | convolution fusion | flops 2098700288 | bytes 35086848 | tf_op jit(solution)/shard_map/td,vd->tv/dot_general | solution.py:104
  144.3 0.1 broadcast_select_fusion
  144.4 22.2 %pmax.7 = f32[2,64]{1,0:T(2,128)S(1)} all-reduce(f32[2,64]{1,0:T(2,128)S(1)} %broadcast_select_fusion), channel_id=1, replica_groups=mesh['dp'=1,'tp'=2,'role'=4] {'tp','role'}, use_global_device_ids=true, to_apply=%region_9.10 | all-reduce | flops 128 | bytes 1024 | tf_op jit(solution)/shard_map/pmax | solution.py:45
  166.6 0.5 exponential_reduce_fusion
  167.1 0.1 broadcast_multiply_fusion.2
  167.1 23.2 %psum.30 = f32[2,64]{1,0:T(2,128)S(1)} all-reduce(f32[2,64]{1,0:T(2,128)S(1)} %broadcast_multiply_fusion.2), channel_id=1, replica_groups=mesh['dp'=1,'tp'=2,'role'=4] {'tp','role'}, use_global_device_ids=true, to_apply=%region_11.12 | all-reduce | flops 128 | bytes 1024 | tf_op jit(solution)/shard_map/psum | solution.py:39
  190.4 1.5 broadcast_subtract_fusion
  191.9 1.3 collective-permute-start
  193.2 0.0 copy-start.5
  193.2 0.0 copy-start.1
  193.3 46.4 %collective-permute-done = f32[64,8000]{1,0:T(8,128)} collective-permute-done((f32[64,8000]{1,0:T(8,128)}, f32[64,8000]{1,0:T(8,128)}, u32[]{:S(2)}, u32[]{:S(2)}) %collective-permute-start) | collective-permute-done | bytes 2048032 | tf_op jit(solution)/shard_map/ppermute | solution.py:108
  239.7 0.0 copy-done.6
  239.7 3.0 %multiply_reduce_fusion = (f32[64]{0:T(128)S(1)}, f32[64]{0:T(128)S(1)}) fusion(f32[64,8000]{1,0:T(8,128)} %collective-permute-done, s32[64]{0:T(128)S(1)} %copy-done.6, s32[8000]{0:T(1024)S(1)} %iota_add_fusion, f32[64,8000]{1,0:T(8,128)} %copy-done.2, f32[64]{0:T(128)S(1)} %fusion.79), kind=kLoop, calls=%fused_computation.4 | loop fusion | flops 3583872 | bytes 4129024 | tf_op jit(solution)/shard_map/reduce_sum | solution.py:109
  242.7 22.3 %psum.31 = f32[2,64]{1,0:T(2,128)S(1)} all-reduce(f32[2,64]{1,0:T(2,128)S(1)} %maximum_multiply_fusion), channel_id=1, replica_groups=mesh['dp'=1,'tp'=2,'role'=4] {'tp','role'}, use_global_device_ids=true, to_apply=%region_14.15 | all-reduce | flops 128 | bytes 1024 | tf_op jit(solution)/shard_map/psum | solution.py:114
  265.0 0.5 bitcast_multiply_fusion
  265.5 0.0 copy-done.1
  (19 shorter events, 0.1 us)
Async XLA Ops:
  7.2 7.8 %copy-start = (bf16[512,2048]{1,0:T(8,128)(2,1)S(1)}, bf16[512,2048]{1,0:T(8,128)(2,1)}, u32[]{:S(2)}) copy-start(bf16[512,2048]{1,0:T(8,128)(2,1)} %param.21) | copy-start | bytes 6291460
  7.2 61.5 %all-reduce.3.cloned.1.call-start = ((), (), s32[]{:S(2)}) async-start(), calls=%async_computation | async-start | bytes 2097152 | tf_op jit(solution)/shard_map/psum | solution.py:39
  13.5 3.6 %copy-start.4 = (bf16[2,64,2048]{2,1,0:T(8,128)(2,1)S(1)}, bf16[2,64,2048]{2,1,0:T(8,128)(2,1)}, u32[]{:S(2)}) copy-start(bf16[2,64,2048]{2,1,0:T(8,128)(2,1)} %param.16) | copy-start | bytes 1572868
  16.8 2.0 copy-start.3
  20.5 107.3 %all-reduce.5.cloned.1.call-start = ((), (), s32[]{:S(2)}) async-start(), calls=%async_computation.1 | async-start | bytes 2097152 | tf_op jit(solution)/shard_map/psum | solution.py:39
  144.3 47.6 %copy-start.2 = (f32[64,8000]{1,0:T(8,128)}, f32[64,8000]{1,0:T(8,128)S(1)}, u32[]{:S(2)}) copy-start(f32[64,8000]{1,0:T(8,128)S(1)} %get-tuple-element.22) | copy-start | bytes 6144004
  167.1 72.6 %copy-start.6 = (s32[64]{0:T(128)S(1)}, s32[64]{0:T(128)}, u32[]{:S(2)}) copy-start(s32[64]{0:T(128)} %param.19) | copy-start | bytes 772
  191.9 47.7 %collective-permute-start = (f32[64,8000]{1,0:T(8,128)}, f32[64,8000]{1,0:T(8,128)}, u32[]{:S(2)}, u32[]{:S(2)}) collective-permute-start(f32[64,8000]{1,0:T(8,128)} %broadcast_subtract_fusion), channel_id=1, source_target_pairs={{2,0},{3,1},{6,4},{7,5}} | collective-permute-start | bytes 6144008 | tf_op jit(solution)/shard_map/ppermute | solution.py:108
  193.2 71.7 %copy-start.5 = (s32[64]{0:T(128)S(1)}, s32[64]{0:T(128)}, u32[]{:S(2)}) copy-start(s32[64]{0:T(128)} %param.18) | copy-start | bytes 772
  193.2 72.3 %copy-start.1 = (bf16[512,2048]{1,0:T(8,128)(2,1)S(1)}, bf16[512,2048]{1,0:T(8,128)(2,1)}, u32[]{:S(2)}) copy-start(bf16[512,2048]{1,0:T(8,128)(2,1)} %param.21) | copy-start | bytes 6291460
Sparse Core Ops, SparseCore 0:
  20.6 48.0 all-reduce.2
  83.2 44.5 all-reduce.4
where the time goes:
time: 273 us; the launch traced here: 272 us
  waiting for transfers between devices  139 us (51%)
  blocking collectives  67.7 us (25%)
  matrix products  32.6 us (12%)
  other arithmetic  15.4 us (6%)
  between operations  15 us (5%)
    psum x2, waiting for transfers between devices, half_sum(): reduced = lax.psum(slot_pick * partial_vals[None], MODEL_AXES)  92.8 us
    ppermute x1, waiting for transfers between devices, per_device(): ref_log_probs = lax.ppermute(log_probs, 'role', back_pairs)  46.4 us
    psum x1, blocking collectives, half_sum(): reduced = lax.psum(slot_pick * partial_vals[None], MODEL_AXES)  23.2 us
    psum x1, blocking collectives, per_device(): lax.psum(jnp.stack([kl_local, tgt_local]) * on_policy, MODEL_AXES)  22.3 us
    pmax x1, blocking collectives, half_max(): lax.pmax(jnp.where(slot_pick, partial_vals[None], -jnp.inf), MODEL_AXES)  22.2 us
    dot_general x1, matrix products, per_device(): jnp.einsum('td,vd->tv', final_rows, w_head, preferred_element_type=jnp.fl...  15.3 us
    dot_general x1, matrix products, last_layer(): jnp.dot(act_vals, w_down, preferred_element_type=jnp.float32)  7.43 us
  transfers between devices with their start and end apart: 3, of which 3 were waited for; matrix products, arithmetic and copies ran while one was open for 0% of the time, Pallas kernels for 0%

commit v1 on v0

v1 whole, which is shorter than its diff:
```python
import functools
import math

import jax
import jax.numpy as jnp
from jax import lax
from jax.experimental import pallas as pl
from jax.experimental.pallas import tpu as pltpu
from jax.sharding import PartitionSpec as P

EPS = 1e-6
ROPE_BASE = 1000000.0
TEMPERATURE = 0.7
NEG = -1e30
GROUPS = 2
CHUNK = 512
LAG = 3
F32 = jnp.float32
BF16 = jnp.bfloat16
MESH = pl.DeviceIdType.MESH


def dot_t(rows, weight):
    return lax.dot_general(rows, weight, (((1,), (1,)), ((), ())), preferred_element_type=F32)


def dot_n(rows, weight):
    return lax.dot_general(rows, weight, (((1,), (0,)), ((), ())), preferred_element_type=F32)


def normed(vals, gain):
    inv_rms = lax.rsqrt(jnp.mean(vals * vals, axis=-1, keepdims=True) + EPS)
    return (vals * inv_rms * gain).astype(BF16)


def kernel(cfg, hidden, gains, w_query, w_key, w_value, w_out, w_gate, w_up, w_down, w_head,
           seg_ref, mask_ref, tgt_ref, bq_ref, bk_ref, bv_ref, out_ref,
           xb, gn, wqkv, wo, wg, wu, wd, wh, qs, os_, part, rbuf, sbuf, ybuf, resid, full,
           zsend, zkeep, zrecv, m_own, s_own, m_kl, s_kl, t_acc, dup, pack,
           in_sem, head_sem, d_send, d_recv, y_send, y_recv, b_send, b_recv, z_send, z_recv, p_send, p_recv):
    tokens, dim, head_dim, q_heads, vocab = cfg
    n = tokens // GROUPS
    own = n // 2
    halves = ((vocab // CHUNK + 2) // 2) * CHUNK
    steps = halves // CHUNK
    tp = lax.axis_index("tp")
    role = lax.axis_index("role")
    core = role % 2
    half = role // 2
    here = role * 2 + tp
    shard = core * 2 + tp
    d_peer = {"role": half * 2 + 1 - core}
    y_peer = {"tp": 1 - tp}
    x_peer = {"role": (1 - half) * 2 + core}
    send_half = 1 - half

    barrier = pltpu.get_barrier_semaphore()
    for hop in range(1, 8):
        other = (here + hop) % 8
        pl.semaphore_signal(barrier, inc=1, device_id={"tp": other % 2, "role": other // 2}, device_id_type=MESH)

    first = []
    kv_rows = pl.ds(pl.multiple_of(tp * head_dim, head_dim), head_dim)
    q_rows = q_heads * head_dim
    moves = [(hidden.at[half], xb), (gains.at[half], gn), (w_query, wqkv.at[pl.ds(0, q_rows)])]
    for slot in range(2):
        moves.append((w_key.at[kv_rows], wqkv.at[pl.ds(q_rows + slot * head_dim, head_dim)]))
        moves.append((w_value.at[kv_rows], wqkv.at[pl.ds(q_rows + (2 + slot) * head_dim, head_dim)]))
    moves += [(w_out, wo), (w_gate, wg), (w_up, wu), (w_down, wd)]
    for idx, (src, dst) in enumerate(moves):
        first.append(pltpu.make_async_copy(src, dst, in_sem.at[idx]))
    for copy in first:
        copy.start()

    def chunk_start(part_half, step):
        nominal = part_half * halves + step * CHUNK
        start = jnp.minimum(nominal, vocab - CHUNK)
        return start, nominal - start

    def head_copy(part_half, step):
        start, _ = chunk_start(part_half, step)
        slot = part_half * steps + step
        return pltpu.make_async_copy(w_head.at[pl.ds(pl.multiple_of(start, 64), CHUNK)], wh.at[slot], head_sem.at[slot])

    @pl.loop(0, steps)
    def _(step):
        head_copy(send_half, step).start()
        head_copy(1 - send_half, step).start()

    ti = lax.broadcasted_iota(jnp.int32, (tokens, tokens), 0)
    tj = lax.broadcasted_iota(jnp.int32, (tokens, tokens), 1)
    eye = ti == tj
    seg_row = seg_ref[...].astype(F32)
    seg_col = jnp.sum(jnp.where(eye, seg_row, 0.0), axis=1, keepdims=True)
    same = seg_col == seg_row
    allowed = same & (ti >= tj)
    seg_first = jnp.min(jnp.where(same, tj.astype(F32), 1e9), axis=1, keepdims=True)
    pos = lax.broadcasted_iota(jnp.int32, (tokens, 1), 0).astype(F32) - seg_first
    wide = 2 * head_dim
    lane = lax.broadcasted_iota(jnp.int32, (1, wide), 1)
    half_dim = head_dim // 2
    freq = jnp.exp((lane % half_dim).astype(F32) * (-2.0 * math.log(ROPE_BASE) / head_dim))
    angles = pos * freq
    cos_t = jnp.cos(angles)
    sin_t = jnp.sin(angles)
    low = (lane % head_dim) < half_dim
    sin_t = jnp.where(low, -sin_t, sin_t)
    even = lane < head_dim
    tgt_col = jnp.sum(jnp.where(eye, tgt_ref[...].astype(F32), 0.0), axis=1, keepdims=True)

    dup[...] = jnp.zeros_like(dup)
    dup[0:q_heads, 0:head_dim] = bq_ref[...].astype(F32)
    dup[q_heads:q_heads + 2, 0:head_dim] = bk_ref[...].astype(F32)
    dup[q_heads + 2:q_heads + 4, 0:head_dim] = bv_ref[...].astype(F32)
    bias = dup[...]
    bias = bias + pltpu.roll(bias, head_dim, 1)
    bias_k = jnp.where(tp == 0, bias[q_heads:q_heads + 1], bias[q_heads + 1:q_heads + 2])
    bias_v = jnp.where(tp == 0, bias[q_heads + 2:q_heads + 3], bias[q_heads + 3:q_heads + 4])

    def rotate(vals):
        turned = jnp.where(low, pltpu.roll(vals, wide - half_dim, 1), pltpu.roll(vals, half_dim, 1))
        return vals * cos_t + turned * sin_t

    first[0].wait()
    first[1].wait()
    xf = xb[...].astype(F32)
    a_in = normed(xf, gn[0:1, :])
    for copy in first[2:7]:
        copy.wait()
    qkv = dot_t(a_in, wqkv[...])
    k_rot = rotate(qkv[:, q_rows:q_rows + wide] + bias_k).astype(BF16)
    v_two = (qkv[:, q_rows + wide:q_rows + 2 * wide] + bias_v).astype(BF16)
    for pair in range(q_heads // 2):
        bias_q = jnp.where(even, bias[2 * pair:2 * pair + 1], bias[2 * pair + 1:2 * pair + 2])
        q_rot = rotate(qkv[:, pair * wide:(pair + 1) * wide] + bias_q) * head_dim ** -0.5
        qs[2 * pair * tokens:(2 * pair + 1) * tokens, :] = jnp.where(even, q_rot, 0.0).astype(BF16)
        qs[(2 * pair + 1) * tokens:(2 * pair + 2) * tokens, :] = jnp.where(even, 0.0, q_rot).astype(BF16)
    scores = dot_t(qs[...], k_rot).reshape(q_heads, tokens, tokens)
    scores = jnp.where(allowed[None], scores, NEG)
    expd = jnp.exp(scores - jnp.max(scores, axis=-1, keepdims=True))
    probs = (expd / jnp.sum(expd, axis=-1, keepdims=True)).astype(BF16).reshape(q_heads * tokens, tokens)
    heads_out = dot_n(probs, v_two)
    for pair in range(q_heads // 2):
        lo = heads_out[2 * pair * tokens:(2 * pair + 1) * tokens]
        hi = heads_out[(2 * pair + 1) * tokens:(2 * pair + 2) * tokens]
        os_[:, pair * wide:(pair + 1) * wide] = jnp.where(even, lo, hi).astype(BF16)
    first[7].wait()
    part[0] = dot_n(os_[...], wo[...])

    def own_rows(grp, which):
        return pl.ds(pl.multiple_of(grp * n + which * own, 8), own)

    def d_copy(red, grp):
        return pltpu.make_async_remote_copy(
            part.at[red, own_rows(grp, 1 - core)], rbuf.at[red, grp], d_send.at[red, grp], d_recv.at[red, grp],
            device_id=d_peer, device_id_type=MESH)

    def y_copy(red, grp):
        return pltpu.make_async_remote_copy(
            sbuf.at[red, grp], ybuf.at[red, grp], y_send.at[red, grp], y_recv.at[red, grp],
            device_id=y_peer, device_id_type=MESH)

    def b_copy(red, grp):
        rows = pl.ds(pl.multiple_of(core * own, 8), own)
        return pltpu.make_async_remote_copy(
            full.at[red, grp, rows], full.at[red, grp, rows], b_send.at[red, grp], b_recv.at[red, grp],
            device_id=d_peer, device_id_type=MESH)

    def chip_sum(red, grp):
        d_copy(red, grp).wait_recv()
        sbuf[red, grp] = part[red, own_rows(grp, core)] + rbuf[red, grp]
        y_copy(red, grp).start()

    def finish(red, grp):
        y_copy(red, grp).wait_recv()
        total = sbuf[red, grp] + ybuf[red, grp]
        if red == 0:
            base = xb[own_rows(grp, core), :].astype(F32)
        else:
            base = resid[grp]
        rows = (base + total).astype(BF16).astype(F32)
        if red == 0:
            resid[grp] = rows
        full[red, grp, pl.ds(pl.multiple_of(core * own, 8), own)] = normed(rows, gn[red + 1:red + 2, :]).astype(F32)
        b_copy(red, grp).start()

    def gathered(red, grp):
        b_copy(red, grp).wait_recv()
        return full[red, grp].astype(BF16)

    def mlp(grp, b_in):
        if grp == 0:
            for copy in first[8:11]:
                copy.wait()
        gate = dot_t(b_in, wg[...])
        up = dot_t(b_in, wu[...])
        act = (gate * (1.0 / (1.0 + jnp.exp(-gate))) * up).astype(BF16)
        part[1, grp * n:(grp + 1) * n] = dot_n(act, wd[...])
        d_copy(1, grp).start()

    pl.semaphore_wait(barrier, 7)
    for grp in range(GROUPS):
        d_copy(0, grp).start()
    for grp in range(GROUPS):
        chip_sum(0, grp)
    finish(0, 0)
    for grp in range(GROUPS):
        mlp(grp, gathered(0, grp))
        if grp + 1 < GROUPS:
            finish(0, grp + 1)
        chip_sum(1, grp)
    finish(1, 0)

    for stat in (s_own, s_kl, t_acc):
        stat[...] = jnp.zeros_like(stat)
    m_own[...] = jnp.full_like(m_own, NEG)
    m_kl[...] = jnp.full_like(m_kl, NEG)
    lanes = lax.broadcasted_iota(jnp.int32, (1, CHUNK), 1)
    tiles = CHUNK // 128

    def z_copy(grp, step):
        return pltpu.make_async_remote_copy(
            zsend.at[grp, step], zrecv.at[grp, step], z_send.at[grp, step], z_recv.at[grp, step],
            device_id=x_peer, device_id_type=MESH)

    def logits(grp, rows, part_half, step):
        start, repeated = chunk_start(part_half, step)
        z = dot_t(rows, wh[part_half * steps + step]) * (1.0 / TEMPERATURE)
        fresh = lanes >= repeated
        z = jnp.where(fresh, z, NEG)
        ids = (lanes + (shard * vocab + start)).astype(F32)
        hit = jnp.where((ids == tgt_col[grp * n:(grp + 1) * n]) & fresh, z, 0.0)
        pieces = [z[:, 128 * t:128 * (t + 1)] for t in range(tiles)]
        m_old = m_own[grp]
        m_new = functools.reduce(jnp.maximum, pieces, m_old)
        total = s_own[grp] * jnp.exp(m_old - m_new)
        for piece in pieces:
            total = total + jnp.exp(piece - m_new)
        m_own[grp] = m_new
        s_own[grp] = total
        t_acc[grp] = t_acc[grp] + functools.reduce(jnp.add, [hit[:, 128 * t:128 * (t + 1)] for t in range(tiles)])
        return z

    def kl_step(grp, step):
        z_copy(grp, step).wait_recv()
        mine, theirs = zkeep[grp, step], zrecv[grp, step]
        diff = mine - theirs
        policy = half == 0
        top = jnp.where(policy, mine, theirs)
        diff = jnp.where(policy, diff, -diff)
        pieces = [top[:, 128 * t:128 * (t + 1)] for t in range(tiles)]
        m_old = m_kl[grp]
        m_new = functools.reduce(jnp.maximum, pieces, m_old)
        total = s_kl[grp] * jnp.exp(m_old - m_new)
        for t, piece in enumerate(pieces):
            total = total + jnp.exp(piece - m_new) * diff[:, 128 * t:128 * (t + 1)]
        m_kl[grp] = m_new
        s_kl[grp] = total

    def head_steps(grp, rows, begin, end):
        @pl.loop(begin, end)
        def _(step):
            if grp == 0:
                head_copy(send_half, step).wait()
            zsend[grp, step] = logits(grp, rows, send_half, step)
            z_copy(grp, step).start()
            if grp == 0:
                head_copy(1 - send_half, step).wait()
            zkeep[grp, step] = logits(grp, rows, 1 - send_half, step)
            if grp > 0:
                @pl.when(step < LAG)
                def _():
                    kl_step(grp - 1, steps - LAG + step)

            @pl.when(step >= LAG)
            def _():
                kl_step(grp, step - LAG)

    middle = steps // 2
    for grp in range(GROUPS):
        rows = gathered(1, grp)
        head_steps(grp, rows, 0, middle)
        if grp + 1 < GROUPS:
            finish(1, grp + 1)
        head_steps(grp, rows, middle, steps)

    def to_row(col):
        return jnp.sum(jnp.where(eye, col, 0.0), axis=0, keepdims=True)

    def stat_rows(m_ref, s_ref):
        m_all = m_ref[...].reshape(tokens, 128)
        m_col = jnp.max(m_all, axis=1, keepdims=True)
        s_col = jnp.sum(s_ref[...].reshape(tokens, 128) * jnp.exp(m_all - m_col), axis=1, keepdims=True)
        return to_row(m_col), to_row(s_col)

    pack[here, 0:1, 0:tokens], pack[here, 1:2, 0:tokens] = stat_rows(m_own, s_own)
    pack[here, 4:5, 0:tokens] = to_row(jnp.sum(t_acc[...].reshape(tokens, 128), axis=1, keepdims=True))
    for step in range(steps - LAG, steps):
        kl_step(GROUPS - 1, step)
    pack[here, 2:3, 0:tokens], pack[here, 3:4, 0:tokens] = stat_rows(m_kl, s_kl)

    def p_copy(hop):
        other = (here + hop) % 8
        return pltpu.make_async_remote_copy(
            pack.at[here], pack.at[here], p_send.at[hop - 1], p_recv.at[hop - 1],
            device_id={"tp": other % 2, "role": other // 2}, device_id_type=MESH)

    for hop in range(1, 8):
        p_copy(hop).start()
    for red in range(2):
        for grp in range(GROUPS):
            d_copy(red, grp).wait_send()
            y_copy(red, grp).wait_send()
            b_copy(red, grp).wait_send()

    @pl.loop(0, GROUPS * steps)
    def _(idx):
        z_copy(idx // steps, idx % steps).wait_send()

    for hop in range(1, 8):
        p_copy(hop).wait_recv()

    def lse(devices):
        tops = [pack[dev, 0:1, 0:tokens] for dev in devices]
        top = functools.reduce(jnp.maximum, tops)
        total = functools.reduce(jnp.add, [pack[dev, 1:2, 0:tokens] * jnp.exp(t - top) for dev, t in zip(devices, tops)])
        return top + jnp.log(total)

    lse_pol = lse(range(4))
    lse_ref = lse(range(4, 8))
    cross = functools.reduce(jnp.add, [pack[dev, 3:4, 0:tokens] * jnp.exp(pack[dev, 2:3, 0:tokens] - lse_pol) for dev in range(8)])
    tgt_z = functools.reduce(jnp.add, [pack[dev, 4:5, 0:tokens] for dev in range(4)])
    mask_vals = mask_ref[...].astype(F32)
    out_ref[0:1, :] = (cross - lse_pol + lse_ref) * mask_vals
    out_ref[1:2, :] = (tgt_z - lse_pol) * mask_vals
    for hop in range(1, 8):
        p_copy(hop).wait_send()


def solution(mesh):
    by_shard = P(("role", "tp"), None)
    by_role = P("role", None)

    def per_device(hidden, segment_ids, loss_mask, target, norm_gains, w_query, b_query, w_key, b_key, w_value, b_value, w_out, w_gate, w_up, w_down, w_head):
        tokens, dim = hidden.shape[1:]
        q_heads, head_dim = b_query.shape
        ff = w_gate.shape[0]
        vocab = w_head.shape[0]
        n = tokens // GROUPS
        own = n // 2
        halves = ((vocab // CHUNK + 2) // 2) * CHUNK
        steps = halves // CHUNK
        any_spec = pl.BlockSpec(memory_space=pl.ANY)
        vmem_spec = pl.BlockSpec(memory_space=pltpu.VMEM)
        wide = 2 * head_dim
        out = pl.pallas_call(
            functools.partial(kernel, (tokens, dim, head_dim, q_heads, vocab)),
            out_shape=jax.ShapeDtypeStruct((2, tokens), F32),
            in_specs=[any_spec] * 10 + [vmem_spec] * 6,
            out_specs=vmem_spec,
            scratch_shapes=[
                pltpu.VMEM((tokens, dim), BF16),
                pltpu.VMEM((3, dim), F32),
                pltpu.VMEM((q_heads * head_dim + 2 * wide, dim), BF16),
                pltpu.VMEM((q_heads * head_dim, dim), BF16),
                pltpu.VMEM((ff, dim), BF16),
                pltpu.VMEM((ff, dim), BF16),
                pltpu.VMEM((ff, dim), BF16),
                pltpu.VMEM((2 * steps, CHUNK, dim), BF16),
                pltpu.VMEM((q_heads * tokens, wide), BF16),
                pltpu.VMEM((tokens, q_heads * head_dim), BF16),
                pltpu.VMEM((2, tokens, dim), F32),
                pltpu.VMEM((2, GROUPS, own, dim), F32),
                pltpu.VMEM((2, GROUPS, own, dim), F32),
                pltpu.VMEM((2, GROUPS, own, dim), F32),
                pltpu.VMEM((GROUPS, own, dim), F32),
                pltpu.VMEM((2, GROUPS, n, dim), F32),
                pltpu.VMEM((GROUPS, steps, n, CHUNK), F32),
                pltpu.VMEM((GROUPS, steps, n, CHUNK), F32),
                pltpu.VMEM((GROUPS, steps, n, CHUNK), F32),
                pltpu.VMEM((GROUPS, n, 128), F32),
                pltpu.VMEM((GROUPS, n, 128), F32),
                pltpu.VMEM((GROUPS, n, 128), F32),
                pltpu.VMEM((GROUPS, n, 128), F32),
                pltpu.VMEM((GROUPS, n, 128), F32),
                pltpu.VMEM((16, 128), F32),
                pltpu.VMEM((8, 8, 128), F32),
                pltpu.SemaphoreType.DMA((11,)),
                pltpu.SemaphoreType.DMA((2 * steps,)),
                pltpu.SemaphoreType.DMA((2, GROUPS)),
                pltpu.SemaphoreType.DMA((2, GROUPS)),
                pltpu.SemaphoreType.DMA((2, GROUPS)),
                pltpu.SemaphoreType.DMA((2, GROUPS)),
                pltpu.SemaphoreType.DMA((2, GROUPS)),
                pltpu.SemaphoreType.DMA((2, GROUPS)),
                pltpu.SemaphoreType.DMA((GROUPS, steps)),
                pltpu.SemaphoreType.DMA((GROUPS, steps)),
                pltpu.SemaphoreType.DMA((7,)),
                pltpu.SemaphoreType.DMA((7,)),
            ],
            compiler_params=pltpu.CompilerParams(
                collective_id=0, has_side_effects=True, vmem_limit_bytes=67043328),
            name="layer_head_kl",
        )(hidden, norm_gains, w_query, w_key, w_value, w_out, w_gate, w_up, w_down, w_head,
          segment_ids.reshape(1, tokens), loss_mask.reshape(1, tokens), target.reshape(1, tokens), b_query, b_key, b_value)
        return out[0], out[1]

    in_specs = (P(None, "dp", None), P("dp"), P("dp"), P("dp"), P(None, None, None), by_shard, by_shard, by_role, by_role, by_role, by_role, by_shard, by_shard, by_shard, by_shard, by_shard)
    return jax.shard_map(per_device, mesh=mesh, in_specs=in_specs, out_specs=(P("dp"), P("dp")), check_vma=False)
```

time: 273 us -> 63.1 us (0.23)
  waiting for transfers between devices: 139 us -> 0 us
  blocking collectives: 67.7 us -> 0 us
  Pallas kernels: 0 us -> 59.6 us
  matrix products: 32.6 us -> 0 us
  other arithmetic: 15.4 us -> 0 us
  between operations: 15 us -> 0.64 us
    psum x2 -> x0, waiting for transfers between devices: 92.8 us -> none  [half_sum(): reduced = lax.psum(slot_pick * partial_vals[None], MODEL_AXES)]
    pallas_call x0 -> x1, Pallas kernels: none -> 59.6 us  [per_device(): pl.pallas_call(functools.partial(kernel, (tokens, dim, head_dim, q_heads,...]
    ppermute x1 -> x0, waiting for transfers between devices: 46.4 us -> none  [per_device(): ref_log_probs = lax.ppermute(log_probs, 'role', back_pairs)]
    psum x2 -> x0, blocking collectives: 45.5 us -> none  [the longest x1 23.2 us: half_sum(): reduced = lax.psum(slot_pick * partial_vals[None], MODEL_AXES)]
    dot_general x8 -> x0, matrix products: 32.6 us -> none  [the longest x1 15.3 us: per_device(): jnp.einsum('td,vd->tv', final_rows, w_head, preferred_element_type=jnp.fl...]
    pmax x1 -> x0, blocking collectives: 22.2 us -> none  [half_max(): lax.pmax(jnp.where(slot_pick, partial_vals[None], -jnp.inf), MODEL_AXES)]
    reduce_sum x6 -> x0, other arithmetic: 7.19 us -> none  [the longest x3 3.66 us: rms_norm(): jnp.mean(vals_f32 * vals_f32, axis=-1, keepdims=True) + EPS]
    mul x5 -> x0, other arithmetic: 3.01 us -> none  [the longest x3 2.48 us: half_sum(): reduced = lax.psum(slot_pick * partial_vals[None], MODEL_AXES)]
  transfers between devices with their start and end apart: 3 -> 0, of which waited for: 3 -> 0; matrix products, arithmetic and copies ran while one was open for 0% -> 0% of each run, Pallas kernels for 0% -> 0%
where the time goes in v1:
time: 63.1 us; the launch traced here: 62.9 us
  Pallas kernels  59.6 us (94%)
  local copies, waits for them, and re-layouts  2.68 us (4%)
  between operations  0.64 us (1%)
    pallas_call x1, Pallas kernels, per_device(): pl.pallas_call(functools.partial(kernel, (tokens, dim, head_dim, q_heads,...  59.6 us
    unnamed x1, local copies, waits for them, and re-layouts  1.45 us

profile of v1, /device:TPU:0, one launch (start us, length us, event | category | flops | bytes accessed | tf_op | source)
XLA Modules:
  0.0 62.9 jit_solution(4695625503224773229)
XLA Ops:
  0.6 1.5 %copy.18.gains = f32[2,3,2048]{2,1,0:T(4,128)} copy(f32[2,3,2048]{2,0,1:T(2,128)} %param.20) | data formatting | bytes 98304 | tf_op args[4]
  2.1 59.6 %layer_head_kl.1 = f32[2,64]{1,0:T(2,128)} custom-call(bf16[2,64,2048]{2,1,0:T(8,128)(2,1)} %hidden.1, f32[2,3,2048]{2,1,0:T(4,128)} %copy.18.gains, bf16[512,2048]{1,0:T(8,128)(2,1)} %w_query.1, bf16[128,2048]{1,0:T(8,128)(2,1)} %w_key.1, bf16[128,2048]{1,0:T(8,128)(2,1)} %w_value.1, bf16[512,2048]{1,0:T(8,128)(2,1)} %w_out.1, bf16[1408,2048]{1,0:T(8,128)(2,1)} %w_gate.1, ...), custom_call_target="tpu_custom_call" | custom-call | tf_op jit(solution)/shard_map/layer_head_kl/pallas_call | solution.py:356
  61.7 1.2 %slice_bitcast_fusion = (f32[64]{0:T(128)}, f32[64]{0:T(128)}) fusion(f32[2,64]{1,0:T(2,128)} %layer_head_kl.1), kind=kLoop, calls=%fused_computation | loop fusion | bytes 1024 | tf_op jit(solution)/shard_map/squeeze | solution.py:406

commit v2 on v0

v2 whole, which is shorter than its diff:
```python
import contextlib
import functools
import math

import jax
import jax.numpy as jnp
from jax import lax
from jax.experimental import pallas as pl
from jax.experimental.pallas import tpu as pltpu
from jax.sharding import PartitionSpec as P

EPS = 1e-6
ROPE_BASE = 1000000.0
TEMPERATURE = 0.7
NEG = -1e30
SIZES = (32, 32)
CHUNK = 512
LAG = 5
F32 = jnp.float32
BF16 = jnp.bfloat16
MESH = pl.DeviceIdType.MESH


def scope(name):
    return contextlib.nullcontext()


def dot_t(rows, weight):
    return lax.dot_general(rows, weight, (((1,), (1,)), ((), ())), preferred_element_type=F32)


def dot_n(rows, weight):
    return lax.dot_general(rows, weight, (((1,), (0,)), ((), ())), preferred_element_type=F32)


def normed(vals, gain):
    inv_rms = lax.rsqrt(jnp.mean(vals * vals, axis=-1, keepdims=True) + EPS)
    return (vals * inv_rms * gain).astype(BF16)


def kernel(cfg, hidden, gains, w_query, w_key, w_value, w_out, w_gate, w_up, w_down, w_head,
           seg_in, mask_in, tgt_in, bq_in, bk_in, bv_in, out_ref,
           xb, gn, seg_ref, mask_ref, tgt_ref, bq_ref, bk_ref, bv_ref, wqkv, wo, wg, wu, wd, wh, xcol, qs, os_, part, rbuf, ybuf, full,
           zsend, zkeep, zrecv, m_own, s_own, m_kl, s_kl, t_acc, dup, pack,
           in_sem, head_sem, d_send, d_recv, y_send, y_recv, b_send, b_recv, z_send, z_recv, p_send, p_recv):
    tokens, dim, head_dim, q_heads, vocab = cfg
    offs = [sum(SIZES[:grp]) for grp in range(len(SIZES))]
    groups = len(SIZES)
    cols = dim // 2
    halves = ((vocab // CHUNK + 2) // 2) * CHUNK
    steps = halves // CHUNK
    tp = lax.axis_index("tp")
    role = lax.axis_index("role")
    core = role % 2
    half = role // 2
    here = role * 2 + tp
    shard = core * 2 + tp
    d_peer = {"role": half * 2 + 1 - core}
    y_peer = {"tp": 1 - tp}
    x_peer = {"role": (1 - half) * 2 + core}
    send_half = 1 - half
    q_rows = q_heads * head_dim
    wide = 2 * head_dim

    kv_rows = pl.ds(pl.multiple_of(tp * head_dim, head_dim), head_dim)
    theirs_cols = pl.ds(pl.multiple_of((1 - core) * cols, cols), cols)
    mine_cols = pl.ds(pl.multiple_of(core * cols, cols), cols)
    moves = [(hidden.at[half], xb), (gains, gn), (seg_in, seg_ref), (mask_in, mask_ref), (tgt_in, tgt_ref),
             (bq_in, bq_ref), (bk_in, bk_ref), (bv_in, bv_ref)]
    n_small = len(moves)
    for piece in range(4):
        rows = pl.ds(piece * q_rows // 4, q_rows // 4)
        moves.append((w_query.at[rows], wqkv.at[rows]))
    for slot in range(2):
        moves.append((w_key.at[kv_rows], wqkv.at[pl.ds(q_rows + slot * head_dim, head_dim)]))
        moves.append((w_value.at[kv_rows], wqkv.at[pl.ds(q_rows + (2 + slot) * head_dim, head_dim)]))
    n_qkv = len(moves)
    moves += [(w_out.at[:, theirs_cols], wo.at[0]), (w_out.at[:, mine_cols], wo.at[1])]
    n_out = len(moves)
    moves += [(w_gate, wg), (w_up, wu), (w_down.at[:, theirs_cols], wd.at[0]), (w_down.at[:, mine_cols], wd.at[1])]
    loads = [pltpu.make_async_copy(src, dst, in_sem.at[idx]) for idx, (src, dst) in enumerate(moves)]
    for copy in loads[:n_out]:
        copy.start()

    barrier = pltpu.get_barrier_semaphore()
    for hop in range(1, 8):
        other = (here + hop) % 8
        pl.semaphore_signal(barrier, inc=1, device_id={"tp": other % 2, "role": other // 2}, device_id_type=MESH)

    def chunk_start(part_half, step):
        nominal = part_half * halves + step * CHUNK
        start = jnp.minimum(nominal, vocab - CHUNK)
        return start, nominal - start

    def head_copy(keep, step):
        start, _ = chunk_start((1 - send_half) if keep else send_half, step)
        return pltpu.make_async_copy(w_head.at[pl.ds(pl.multiple_of(start, 64), CHUNK)],
                                     wh.at[step, pl.ds(keep * CHUNK, CHUNK)], head_sem.at[keep, step])

    ti = lax.broadcasted_iota(jnp.int32, (tokens, tokens), 0)
    tj = lax.broadcasted_iota(jnp.int32, (tokens, tokens), 1)
    eye = ti == tj
    lane = lax.broadcasted_iota(jnp.int32, (1, wide), 1)
    half_dim = head_dim // 2
    freq = jnp.exp((lane % half_dim).astype(F32) * (-2.0 * math.log(ROPE_BASE) / head_dim))
    low = (lane % head_dim) < half_dim
    even = lane < head_dim

    def gain_row(which):
        return jnp.where(half == 0, gn[which, 0:1, :], gn[which, 1:2, :])

    with scope("wait_x"):
        for copy in loads[:n_small]:
            copy.wait()
    with scope("norm_x"):
        seg_row = seg_ref[...].astype(F32)
        seg_col = jnp.sum(jnp.where(eye, seg_row, 0.0), axis=1, keepdims=True)
        same = seg_col == seg_row
        allowed = same & (ti >= tj)
        seg_first = jnp.min(jnp.where(same, tj.astype(F32), 1e9), axis=1, keepdims=True)
        pos = lax.broadcasted_iota(jnp.int32, (tokens, 1), 0).astype(F32) - seg_first
        angles = pos * freq
        cos_t = jnp.cos(angles)
        sin_t = jnp.sin(angles)
        sin_t = jnp.where(low, -sin_t, sin_t)
        tgt_col = jnp.sum(jnp.where(eye, tgt_ref[...].astype(F32), 0.0), axis=1, keepdims=True)
        dup[...] = jnp.zeros_like(dup)
        dup[0:q_heads, 0:head_dim] = bq_ref[...].astype(F32)
        dup[q_heads:q_heads + 2, 0:head_dim] = bk_ref[...].astype(F32)
        dup[q_heads + 2:q_heads + 4, 0:head_dim] = bv_ref[...].astype(F32)
        bias = dup[...]
        bias = bias + pltpu.roll(bias, head_dim, 1)
        bias_k = jnp.where(tp == 0, bias[q_heads:q_heads + 1], bias[q_heads + 1:q_heads + 2])
        bias_v = jnp.where(tp == 0, bias[q_heads + 2:q_heads + 3], bias[q_heads + 3:q_heads + 4])
        xf = xb[...].astype(F32)
        xcol[0] = xf[:, :cols]
        xcol[1] = xf[:, cols:]
        a_in = normed(xf, gain_row(0))

    def rotate(vals):
        turned = jnp.where(low, pltpu.roll(vals, wide - half_dim, 1), pltpu.roll(vals, half_dim, 1))
        return vals * cos_t + turned * sin_t

    with scope("wait_qkv"):
        for copy in loads[n_small:n_qkv]:
            copy.wait()
    for copy in loads[n_out:]:
        copy.start()

    @pl.loop(0, steps)
    def _(step):
        head_copy(0, step).start()
        head_copy(1, step).start()

    with scope("qkv"):
        qkv = dot_t(a_in, wqkv[...])
        k_rot = rotate(qkv[:, q_rows:q_rows + wide] + bias_k).astype(BF16)
        v_two = (qkv[:, q_rows + wide:q_rows + 2 * wide] + bias_v).astype(BF16)
        for pair in range(q_heads // 2):
            bias_q = jnp.where(even, bias[2 * pair:2 * pair + 1], bias[2 * pair + 1:2 * pair + 2])
            q_rot = rotate(qkv[:, pair * wide:(pair + 1) * wide] + bias_q) * head_dim ** -0.5
            qs[2 * pair * tokens:(2 * pair + 1) * tokens, :] = jnp.where(even, q_rot, 0.0).astype(BF16)
            qs[(2 * pair + 1) * tokens:(2 * pair + 2) * tokens, :] = jnp.where(even, 0.0, q_rot).astype(BF16)
    with scope("attn"):
        scores = dot_t(qs[...], k_rot).reshape(q_heads, tokens, tokens)
        scores = jnp.where(allowed[None], scores, NEG)
        expd = jnp.exp(scores - jnp.max(scores, axis=-1, keepdims=True))
        probs = (expd / jnp.sum(expd, axis=-1, keepdims=True)).astype(BF16).reshape(q_heads * tokens, tokens)
        heads_out = dot_n(probs, v_two)
        for pair in range(q_heads // 2):
            lo = heads_out[2 * pair * tokens:(2 * pair + 1) * tokens]
            hi = heads_out[(2 * pair + 1) * tokens:(2 * pair + 2) * tokens]
            os_[:, pair * wide:(pair + 1) * wide] = jnp.where(even, lo, hi).astype(BF16)

    def rows_of(grp):
        return pl.ds(offs[grp], SIZES[grp])

    def d_copy(red, grp):
        return pltpu.make_async_remote_copy(
            part.at[red, 0, rows_of(grp)], rbuf.at[red, rows_of(grp)], d_send.at[red, grp], d_recv.at[red, grp],
            device_id=d_peer, device_id_type=MESH)

    def y_copy(red, grp):
        return pltpu.make_async_remote_copy(
            part.at[red, 1, rows_of(grp)], ybuf.at[red, rows_of(grp)], y_send.at[red, grp], y_recv.at[red, grp],
            device_id=y_peer, device_id_type=MESH)

    def b_copy(red, grp):
        return pltpu.make_async_remote_copy(
            full.at[red, core, rows_of(grp)], full.at[red, core, rows_of(grp)], b_send.at[red, grp], b_recv.at[red, grp],
            device_id=d_peer, device_id_type=MESH)

    def chip_sum(red, grp):
        rows = rows_of(grp)
        with scope(f"wait_d{red}{grp}"):
            d_copy(red, grp).wait_recv()
        part[red, 1, rows] = part[red, 1, rows] + rbuf[red, rows]
        y_copy(red, grp).start()

    def finish(red, grp):
        rows = rows_of(grp)
        with scope(f"wait_y{red}{grp}"):
            y_copy(red, grp).wait_recv()
        base = xcol[core, rows] if red == 0 else full[0, core, rows]
        full[red, core, rows] = (base + (part[red, 1, rows] + ybuf[red, rows])).astype(BF16).astype(F32)
        b_copy(red, grp).start()

    def gathered(red, grp):
        rows = rows_of(grp)
        with scope(f"wait_b{red}{grp}"):
            b_copy(red, grp).wait_recv()
        left, right = full[red, 0, rows], full[red, 1, rows]
        total = jnp.sum(left * left, axis=-1, keepdims=True) + jnp.sum(right * right, axis=-1, keepdims=True)
        inv_rms = lax.rsqrt(total * (1.0 / dim) + EPS)
        gain = gain_row(red + 1)
        return jnp.concatenate([(left * inv_rms * gain[:, :cols]).astype(BF16),
                                (right * inv_rms * gain[:, cols:]).astype(BF16)], axis=1)

    def mlp(grp, b_in):
        rows = rows_of(grp)
        if grp == 0:
            for copy in loads[n_out:]:
                copy.wait()
        with scope(f"mlp{grp}"):
            gate = dot_t(b_in, wg[...])
            up = dot_t(b_in, wu[...])
            act = (gate * (1.0 / (1.0 + jnp.exp(-gate))) * up).astype(BF16)
            part[1, 0, rows] = dot_n(act, wd[0])
        d_copy(1, grp).start()
        with scope(f"down{grp}"):
            part[1, 1, rows] = dot_n(act, wd[1])

    for copy in loads[n_qkv:n_out]:
        copy.wait()
    with scope("oproj"):
        part[0, 0] = dot_n(os_[...], wo[0])
    with scope("entry"):
        pl.semaphore_wait(barrier, 7)
    for grp in range(groups):
        d_copy(0, grp).start()
    with scope("oproj"):
        part[0, 1] = dot_n(os_[...], wo[1])
    for grp in range(groups):
        chip_sum(0, grp)
    finish(0, 0)
    for grp in range(groups):
        mlp(grp, gathered(0, grp))
        if grp + 1 < groups:
            finish(0, grp + 1)
        if grp == groups - 1:
            finish(1, 0)
        chip_sum(1, grp)

    for stat in (s_own, s_kl, t_acc):
        stat[...] = jnp.zeros_like(stat)
    m_own[...] = jnp.full_like(m_own, NEG)
    m_kl[...] = jnp.full_like(m_kl, NEG)
    lanes = lax.broadcasted_iota(jnp.int32, (1, CHUNK), 1)
    tiles = CHUNK // 128

    def split(vals):
        return [vals[:, 128 * t:128 * (t + 1)] for t in range(tiles)]

    def z_copy(grp, step):
        return pltpu.make_async_remote_copy(
            zsend.at[step, rows_of(grp)], zrecv.at[step, rows_of(grp)], z_send.at[grp, step], z_recv.at[grp, step],
            device_id=x_peer, device_id_type=MESH)

    def scaled(z, keep, step):
        _, repeated = chunk_start((1 - send_half) if keep else send_half, step)
        return jnp.where(lanes >= repeated, z * (1.0 / TEMPERATURE), NEG)

    def own_step(grp, step):
        rows = rows_of(grp)
        m_old, total, hits = m_own[rows], s_own[rows], t_acc[rows]
        goal = tgt_col[offs[grp]:offs[grp] + SIZES[grp]]
        parts = []
        for keep, src in ((0, zsend), (1, zkeep)):
            start, repeated = chunk_start((1 - send_half) if keep else send_half, step)
            z = src[step, rows]
            ids = (lanes + (shard * vocab + start)).astype(F32)
            for hit in split(jnp.where((ids == goal) & (lanes >= repeated), z, 0.0)):
                hits = hits + hit
            parts += split(z)
        m_new = functools.reduce(jnp.maximum, parts, m_old)
        total = total * jnp.exp(m_old - m_new)
        for piece in parts:
            total = total + jnp.exp(piece - m_new)
        m_own[rows] = m_new
        s_own[rows] = total
        t_acc[rows] = hits

    def kl_wait(grp, step):
        with scope(f"wait_z{grp}"):
            z_copy(grp, step).wait_recv()

    def kl_step(grp, step):
        rows = rows_of(grp)
        mine, theirs = zkeep[step, rows], zrecv[step, rows]
        policy = half == 0
        tops = split(jnp.where(policy, mine, theirs))
        diffs = split(jnp.where(policy, mine - theirs, theirs - mine))
        m_old = m_kl[rows]
        m_new = functools.reduce(jnp.maximum, tops, m_old)
        total = s_kl[rows] * jnp.exp(m_old - m_new)
        for top, diff in zip(tops, diffs):
            total = total + jnp.exp(top - m_new) * diff
        m_kl[rows] = m_new
        s_kl[rows] = total

    def head_step(grp, h_in, step, behind, kl_of):
        rows = rows_of(grp)
        if grp == 0:
            with scope("wait_w"):
                head_copy(0, step).wait()
                head_copy(1, step).wait()
        if kl_of is not None:
            kl_wait(*kl_of)
        with scope(f"step{grp}"):
            z = dot_t(h_in, wh[step])
            zsend[step, rows] = scaled(z[:, :CHUNK], 0, step)
            zkeep[step, rows] = scaled(z[:, CHUNK:], 1, step)
            if behind is not None:
                own_step(*behind)
            if kl_of is not None:
                kl_step(*kl_of)
        z_copy(grp, step).start()

    def first_step(grp, h_in):
        rows = rows_of(grp)
        head_copy(0, 0).wait()
        with scope("first"):
            zsend[0, rows] = scaled(dot_t(h_in, wh[0, 0:CHUNK]), 0, 0)
        z_copy(grp, 0).start()
        head_copy(1, 0).wait()
        with scope("first"):
            zkeep[0, rows] = scaled(dot_t(h_in, wh[0, CHUNK:2 * CHUNK]), 1, 0)

    for grp in range(groups):
        h_in = gathered(1, grp)
        if grp == 0:
            first_step(grp, h_in)

            @pl.loop(1, LAG)
            def _(step):
                head_step(grp, h_in, step, (grp, step - 1), None)
        else:
            head_step(grp, h_in, 0, (grp - 1, steps - 1), (grp - 1, steps - LAG))

            @pl.loop(1, LAG)
            def _(step):
                head_step(grp, h_in, step, (grp, step - 1), (grp - 1, steps - LAG + step))

        if grp + 1 < groups:
            finish(1, grp + 1)

        @pl.loop(LAG, steps)
        def _(step):
            head_step(grp, h_in, step, (grp, step - 1), (grp, step - LAG))

    last = groups - 1
    own_step(last, steps - 1)

    def to_row(col):
        return jnp.sum(jnp.where(eye, col, 0.0), axis=0, keepdims=True)

    def stat_rows(m_ref, s_ref):
        m_all = m_ref[...]
        m_col = jnp.max(m_all, axis=1, keepdims=True)
        s_col = jnp.sum(s_ref[...] * jnp.exp(m_all - m_col), axis=1, keepdims=True)
        return to_row(m_col), to_row(s_col)

    pack[here, 0:1, 0:tokens], pack[here, 1:2, 0:tokens] = stat_rows(m_own, s_own)
    pack[here, 4:5, 0:tokens] = to_row(jnp.sum(t_acc[...], axis=1, keepdims=True))
    for red in range(2):
        for grp in range(groups):
            d_copy(red, grp).wait_send()
            y_copy(red, grp).wait_send()
            b_copy(red, grp).wait_send()
    for step in range(steps - LAG, steps):
        kl_wait(last, step)
        kl_step(last, step)
    pack[here, 2:3, 0:tokens], pack[here, 3:4, 0:tokens] = stat_rows(m_kl, s_kl)

    def p_copy(hop):
        other = (here + hop) % 8
        return pltpu.make_async_remote_copy(
            pack.at[here], pack.at[here], p_send.at[hop - 1], p_recv.at[hop - 1],
            device_id={"tp": other % 2, "role": other // 2}, device_id_type=MESH)

    for hop in range(1, 8):
        p_copy(hop).start()
    for grp in range(groups):
        @pl.loop(0, steps)
        def _(step):
            z_copy(grp, step).wait_send()

    with scope("wait_p"):
        for hop in range(1, 8):
            p_copy(hop).wait_recv()

    with scope("final"):
        def lse(devices):
            tops = [pack[dev, 0:1, 0:tokens] for dev in devices]
            top = functools.reduce(jnp.maximum, tops)
            total = functools.reduce(jnp.add, [pack[dev, 1:2, 0:tokens] * jnp.exp(t - top) for dev, t in zip(devices, tops)])
            return top + jnp.log(total)

        lse_pol = lse(range(4))
        lse_ref = lse(range(4, 8))
        cross = functools.reduce(jnp.add, [pack[dev, 3:4, 0:tokens] * jnp.exp(pack[dev, 2:3, 0:tokens] - lse_pol) for dev in range(8)])
        tgt_z = functools.reduce(jnp.add, [pack[dev, 4:5, 0:tokens] for dev in range(4)])
        mask_vals = mask_ref[...].astype(F32)
        out_ref[0:1, :] = (cross - lse_pol + lse_ref) * mask_vals
        out_ref[1:2, :] = (tgt_z - lse_pol) * mask_vals
    with scope("wait_ps"):
        for hop in range(1, 8):
            p_copy(hop).wait_send()


def solution(mesh):
    by_shard = P(("role", "tp"), None)
    by_role = P("role", None)

    def per_device(hidden, segment_ids, loss_mask, target, norm_gains, w_query, b_query, w_key, b_key, w_value, b_value, w_out, w_gate, w_up, w_down, w_head):
        tokens, dim = hidden.shape[1:]
        q_heads, head_dim = b_query.shape
        ff = w_gate.shape[0]
        vocab = w_head.shape[0]
        groups = len(SIZES)
        cols = dim // 2
        q_rows = q_heads * head_dim
        halves = ((vocab // CHUNK + 2) // 2) * CHUNK
        steps = halves // CHUNK
        wide = 2 * head_dim
        sem = pltpu.SemaphoreType.DMA
        out = pl.pallas_call(
            functools.partial(kernel, (tokens, dim, head_dim, q_heads, vocab)),
            out_shape=jax.ShapeDtypeStruct((2, tokens), F32),
            in_specs=[pl.BlockSpec(memory_space=pl.ANY)] * 16,
            out_specs=pl.BlockSpec(memory_space=pltpu.VMEM),
            scratch_shapes=[
                pltpu.VMEM((tokens, dim), BF16),
                pltpu.VMEM((3, 2, dim), F32),
                pltpu.VMEM((1, tokens), jnp.int32),
                pltpu.VMEM((1, tokens), jnp.int32),
                pltpu.VMEM((1, tokens), jnp.int32),
                pltpu.VMEM(b_query.shape, BF16),
                pltpu.VMEM(b_key.shape, BF16),
                pltpu.VMEM(b_value.shape, BF16),
                pltpu.VMEM((q_rows + 2 * wide, dim), BF16),
                pltpu.VMEM((2, q_rows, cols), BF16),
                pltpu.VMEM((ff, dim), BF16),
                pltpu.VMEM((ff, dim), BF16),
                pltpu.VMEM((2, ff, cols), BF16),
                pltpu.VMEM((steps, 2 * CHUNK, dim), BF16),
                pltpu.VMEM((2, tokens, cols), F32),
                pltpu.VMEM((q_heads * tokens, wide), BF16),
                pltpu.VMEM((tokens, q_rows), BF16),
                pltpu.VMEM((2, 2, tokens, cols), F32),
                pltpu.VMEM((2, tokens, cols), F32),
                pltpu.VMEM((2, tokens, cols), F32),
                pltpu.VMEM((2, 2, tokens, cols), F32),
                pltpu.VMEM((steps, tokens, CHUNK), F32),
                pltpu.VMEM((steps, tokens, CHUNK), F32),
                pltpu.VMEM((steps, tokens, CHUNK), F32),
                pltpu.VMEM((tokens, 128), F32),
                pltpu.VMEM((tokens, 128), F32),
                pltpu.VMEM((tokens, 128), F32),
                pltpu.VMEM((tokens, 128), F32),
                pltpu.VMEM((tokens, 128), F32),
                pltpu.VMEM((16, 128), F32),
                pltpu.VMEM((8, 8, 128), F32),
                sem((22,)), sem((2, steps)),
                sem((2, groups)), sem((2, groups)), sem((2, groups)), sem((2, groups)), sem((2, groups)), sem((2, groups)),
                sem((groups, steps)), sem((groups, steps)), sem((7,)), sem((7,)),
            ],
            compiler_params=pltpu.CompilerParams(
                collective_id=0, has_side_effects=True, vmem_limit_bytes=67043328),
            name="layer_head_kl",
        )(hidden, jnp.transpose(norm_gains, (1, 0, 2)), w_query, w_key, w_value, w_out, w_gate, w_up, w_down, w_head,
          segment_ids.reshape(1, tokens), loss_mask.reshape(1, tokens), target.reshape(1, tokens), b_query, b_key, b_value)
        return out[0], out[1]

    in_specs = (P(None, "dp", None), P("dp"), P("dp"), P("dp"), P(None, None, None), by_shard, by_shard, by_role, by_role, by_role, by_role, by_shard, by_shard, by_shard, by_shard, by_shard)
    return jax.shard_map(per_device, mesh=mesh, in_specs=in_specs, out_specs=(P("dp"), P("dp")), check_vma=False)
```

time: 273 us -> 58.3 us (0.21)
  waiting for transfers between devices: 139 us -> 0 us
  blocking collectives: 67.7 us -> 0 us
  Pallas kernels: 0 us -> 56.3 us
  matrix products: 32.6 us -> 0 us
  other arithmetic: 15.4 us -> 0 us
  between operations: 15 us -> 0.64 us
    psum x2 -> x0, waiting for transfers between devices: 92.8 us -> none  [half_sum(): reduced = lax.psum(slot_pick * partial_vals[None], MODEL_AXES)]
    pallas_call x0 -> x1, Pallas kernels: none -> 56.3 us  [per_device(): pl.pallas_call(functools.partial(kernel, (tokens, dim, head_dim, q_heads,...]
    ppermute x1 -> x0, waiting for transfers between devices: 46.4 us -> none  [per_device(): ref_log_probs = lax.ppermute(log_probs, 'role', back_pairs)]
    psum x2 -> x0, blocking collectives: 45.5 us -> none  [the longest x1 23.2 us: half_sum(): reduced = lax.psum(slot_pick * partial_vals[None], MODEL_AXES)]
    dot_general x8 -> x0, matrix products: 32.6 us -> none  [the longest x1 15.3 us: per_device(): jnp.einsum('td,vd->tv', final_rows, w_head, preferred_element_type=jnp.fl...]
    pmax x1 -> x0, blocking collectives: 22.2 us -> none  [half_max(): lax.pmax(jnp.where(slot_pick, partial_vals[None], -jnp.inf), MODEL_AXES)]
    reduce_sum x6 -> x0, other arithmetic: 7.19 us -> none  [the longest x3 3.66 us: rms_norm(): jnp.mean(vals_f32 * vals_f32, axis=-1, keepdims=True) + EPS]
    mul x5 -> x0, other arithmetic: 3.01 us -> none  [the longest x3 2.48 us: half_sum(): reduced = lax.psum(slot_pick * partial_vals[None], MODEL_AXES)]
  transfers between devices with their start and end apart: 3 -> 0, of which waited for: 3 -> 0; matrix products, arithmetic and copies ran while one was open for 0% -> 0% of each run, Pallas kernels for 0% -> 0%
where the time goes in v2:
time: 58.3 us; the launch traced here: 58.2 us
  Pallas kernels  56.3 us (97%)
  local copies, waits for them, and re-layouts  1.25 us (2%)
  between operations  0.64 us (1%)
    pallas_call x1, Pallas kernels, per_device(): pl.pallas_call(functools.partial(kernel, (tokens, dim, head_dim, q_heads,...  56.3 us
    squeeze x1, local copies, waits for them, and re-layouts, per_device(): return (out[0], out[1])  1.25 us

profile of v2, /device:TPU:0, one launch (start us, length us, event | category | flops | bytes accessed | tf_op | source)
XLA Modules:
  0.0 58.2 jit_solution(363777179231766505)
XLA Ops:
  0.6 56.3 %layer_head_kl.1 = f32[2,64]{1,0:T(2,128)} custom-call(bf16[2,64,2048]{2,1,0:T(8,128)(2,1)} %hidden.1, f32[3,2,2048]{2,1,0:T(2,128)} %bitcast.8, bf16[512,2048]{1,0:T(8,128)(2,1)} %w_query.1, bf16[128,2048]{1,0:T(8,128)(2,1)} %w_key.1, bf16[128,2048]{1,0:T(8,128)(2,1)} %w_value.1, bf16[512,2048]{1,0:T(8,128)(2,1)} %w_out.1, bf16[1408,2048]{1,0:T(8,128)(2,1)} %w_gate.1, ...), custom_call_target="tpu_custom_call" | custom-call | tf_op jit(solution)/shard_map/layer_head_kl/pallas_call | solution.py:437
  56.9 1.3 %slice_bitcast_fusion = (f32[64]{0:T(128)}, f32[64]{0:T(128)}) fusion(f32[2,64]{1,0:T(2,128)} %layer_head_kl.1), kind=kLoop, calls=%fused_computation | loop fusion | bytes 1024 | tf_op jit(solution)/shard_map/squeeze | solution.py:483

commit v3 on v2

--- a/solution.py
+++ b/solution.py
@@ -13,7 +13,10 @@
 ROPE_BASE = 1000000.0
 TEMPERATURE = 0.7
 NEG = -1e30
-SIZES = (32, 32)
+SIZES = (24, 40)
+AHEAD = 4
+LATE = 6
+TILE = 256
 CHUNK = 512
 LAG = 5
 F32 = jnp.float32
@@ -40,13 +43,14 @@
 
 def kernel(cfg, hidden, gains, w_query, w_key, w_value, w_out, w_gate, w_up, w_down, w_head,
            seg_in, mask_in, tgt_in, bq_in, bk_in, bv_in, out_ref,
-           xb, gn, seg_ref, mask_ref, tgt_ref, bq_ref, bk_ref, bv_ref, wqkv, wo, wg, wu, wd, wh, xcol, qs, os_, part, rbuf, ybuf, full,
-           zsend, zkeep, zrecv, m_own, s_own, m_kl, s_kl, t_acc, dup, pack,
+           xb, gn, seg_ref, mask_ref, tgt_ref, bq_ref, bk_ref, bv_ref, wqkv, wo, wgu, wd, wh, xcol, qs, os_, part, rbuf, ybuf, full,
+           gate_up, zsend, zkeep, zrecv, m_own, s_own, m_kl, s_kl, t_acc, dup, pack,
            in_sem, head_sem, d_send, d_recv, y_send, y_recv, b_send, b_recv, z_send, z_recv, p_send, p_recv):
     tokens, dim, head_dim, q_heads, vocab = cfg
     offs = [sum(SIZES[:grp]) for grp in range(len(SIZES))]
     groups = len(SIZES)
     cols = dim // 2
+    ff = w_gate.shape[0]
     halves = ((vocab // CHUNK + 2) // 2) * CHUNK
     steps = halves // CHUNK
     tp = lax.axis_index("tp")
@@ -77,9 +81,11 @@
     n_qkv = len(moves)
     moves += [(w_out.at[:, theirs_cols], wo.at[0]), (w_out.at[:, mine_cols], wo.at[1])]
     n_out = len(moves)
-    moves += [(w_gate, wg), (w_up, wu), (w_down.at[:, theirs_cols], wd.at[0]), (w_down.at[:, mine_cols], wd.at[1])]
+    moves += [(w_gate, wgu.at[pl.ds(0, ff)]), (w_up, wgu.at[pl.ds(ff, ff)])]
+    n_gu = len(moves)
+    moves += [(w_down.at[:, theirs_cols], wd.at[0]), (w_down.at[:, mine_cols], wd.at[1])]
     loads = [pltpu.make_async_copy(src, dst, in_sem.at[idx]) for idx, (src, dst) in enumerate(moves)]
-    for copy in loads[:n_out]:
+    for copy in loads[:n_qkv]:
         copy.start()
 
     barrier = pltpu.get_barrier_semaphore()
@@ -144,7 +150,7 @@
     with scope("wait_qkv"):
         for copy in loads[n_small:n_qkv]:
             copy.wait()
-    for copy in loads[n_out:]:
+    for copy in loads[n_qkv:]:
         copy.start()
 
     @pl.loop(0, steps)
@@ -205,10 +211,12 @@
         full[red, core, rows] = (base + (part[red, 1, rows] + ybuf[red, rows])).astype(BF16).astype(F32)
         b_copy(red, grp).start()
 
-    def gathered(red, grp):
-        rows = rows_of(grp)
+    def b_wait(red, grp):
         with scope(f"wait_b{red}{grp}"):
             b_copy(red, grp).wait_recv()
+
+    def normed_rows(red, off, size):
+        rows = pl.ds(off, size)
         left, right = full[red, 0, rows], full[red, 1, rows]
         total = jnp.sum(left * left, axis=-1, keepdims=True) + jnp.sum(right * right, axis=-1, keepdims=True)
         inv_rms = lax.rsqrt(total * (1.0 / dim) + EPS)
@@ -216,14 +224,43 @@
         return jnp.concatenate([(left * inv_rms * gain[:, :cols]).astype(BF16),
                                 (right * inv_rms * gain[:, cols:]).astype(BF16)], axis=1)
 
+    def gathered(red, grp):
+        b_wait(red, grp)
+        return normed_rows(red, offs[grp], SIZES[grp])
+
+    def turn_tiles(ref, rows):
+        for k in range(dim // TILE):
+            ref[rows, k * TILE:(k + 1) * TILE] = ref[rows, k * TILE:(k + 1) * TILE].T
+
+    def turn(first, last):
+        with scope("turn"):
+            @pl.loop(first, last)
+            def _(blk):
+                turn_tiles(wgu, pl.ds(pl.multiple_of(blk * TILE, TILE), TILE))
+
+    def turn_head(step):
+        for row in range(0, CHUNK, TILE):
+            turn_tiles(wh.at[step], pl.ds(row, TILE))
+
+    def turned_dot(vals, ref, row):
+        return functools.reduce(jnp.add, [dot_n(vals[:, k * TILE:(k + 1) * TILE], ref[row:row + TILE, k * TILE:(k + 1) * TILE])
+                                          for k in range(dim // TILE)])
+
     def mlp(grp, b_in):
         rows = rows_of(grp)
         if grp == 0:
-            for copy in loads[n_out:]:
+            for copy in loads[n_gu:]:
                 copy.wait()
+        if grp == groups - 1:
+            for step in range(AHEAD):
+                head_copy(0, step).wait()
         with scope(f"mlp{grp}"):
-            gate = dot_t(b_in, wg[...])
-            up = dot_t(b_in, wu[...])
+            if grp == groups - 1:
+                for step in range(AHEAD):
+                    turn_head(step)
+            for row in range(0, 2 * ff, TILE):
+                gate_up[rows, row:row + TILE] = turned_dot(b_in, wgu, row)
+            gate, up = gate_up[rows, 0:ff], gate_up[rows, ff:2 * ff]
             act = (gate * (1.0 / (1.0 + jnp.exp(-gate))) * up).astype(BF16)
             part[1, 0, rows] = dot_n(act, wd[0])
         d_copy(1, grp).start()
@@ -240,8 +277,14 @@
         d_copy(0, grp).start()
     with scope("oproj"):
         part[0, 1] = dot_n(os_[...], wo[1])
+    blocks = 2 * ff // TILE
+    early = ff // TILE
     for grp in range(groups):
         chip_sum(0, grp)
+    loads[n_out].wait()
+    turn(0, early)
+    loads[n_out + 1].wait()
+    turn(early, blocks)
     finish(0, 0)
     for grp in range(groups):
         mlp(grp, gathered(0, grp))
@@ -261,19 +304,24 @@
     def split(vals):
         return [vals[:, 128 * t:128 * (t + 1)] for t in range(tiles)]
 
-    def z_copy(grp, step):
+    entries = [(step, offs[grp], SIZES[grp]) for grp in range(groups) for step in range(steps)]
+
+    def z_copy(entry):
+        step, off, size = entries[entry]
+        rows = pl.ds(off, size)
         return pltpu.make_async_remote_copy(
-            zsend.at[step, rows_of(grp)], zrecv.at[step, rows_of(grp)], z_send.at[grp, step], z_recv.at[grp, step],
+            zsend.at[step, rows], zrecv.at[step, rows], z_send.at[entry], z_recv.at[entry],
             device_id=x_peer, device_id_type=MESH)
 
     def scaled(z, keep, step):
         _, repeated = chunk_start((1 - send_half) if keep else send_half, step)
         return jnp.where(lanes >= repeated, z * (1.0 / TEMPERATURE), NEG)
 
-    def own_step(grp, step):
-        rows = rows_of(grp)
+    def own_step(entry):
+        step, off, size = entries[entry]
+        rows = pl.ds(off, size)
         m_old, total, hits = m_own[rows], s_own[rows], t_acc[rows]
-        goal = tgt_col[offs[grp]:offs[grp] + SIZES[grp]]
+        goal = tgt_col[off:off + size]
         parts = []
         for keep, src in ((0, zsend), (1, zkeep)):
             start, repeated = chunk_start((1 - send_half) if keep else send_half, step)
@@ -290,12 +338,13 @@
         s_own[rows] = total
         t_acc[rows] = hits
 
-    def kl_wait(grp, step):
-        with scope(f"wait_z{grp}"):
-            z_copy(grp, step).wait_recv()
-
-    def kl_step(grp, step):
-        rows = rows_of(grp)
+    def kl_wait(entry):
+        with scope(f"wait_z{entry}"):
+            z_copy(entry).wait_recv()
+
+    def kl_step(entry):
+        step, off, size = entries[entry]
+        rows = pl.ds(off, size)
         mine, theirs = zkeep[step, rows], zrecv[step, rows]
         policy = half == 0
         tops = split(jnp.where(policy, mine, theirs))
@@ -308,58 +357,43 @@
         m_kl[rows] = m_new
         s_kl[rows] = total
 
-    def head_step(grp, h_in, step, behind, kl_of):
-        rows = rows_of(grp)
-        if grp == 0:
+    def head_entry(entry, h_in):
+        step, off, size = entries[entry]
+        rows = pl.ds(off, size)
+        if entry == step:
             with scope("wait_w"):
-                head_copy(0, step).wait()
                 head_copy(1, step).wait()
-        if kl_of is not None:
-            kl_wait(*kl_of)
-        with scope(f"step{grp}"):
-            z = dot_t(h_in, wh[step])
-            zsend[step, rows] = scaled(z[:, :CHUNK], 0, step)
-            zkeep[step, rows] = scaled(z[:, CHUNK:], 1, step)
-            if behind is not None:
-                own_step(*behind)
-            if kl_of is not None:
-                kl_step(*kl_of)
-        z_copy(grp, step).start()
-
-    def first_step(grp, h_in):
-        rows = rows_of(grp)
-        head_copy(0, 0).wait()
-        with scope("first"):
-            zsend[0, rows] = scaled(dot_t(h_in, wh[0, 0:CHUNK]), 0, 0)
-        z_copy(grp, 0).start()
-        head_copy(1, 0).wait()
-        with scope("first"):
-            zkeep[0, rows] = scaled(dot_t(h_in, wh[0, CHUNK:2 * CHUNK]), 1, 0)
-
-    for grp in range(groups):
-        h_in = gathered(1, grp)
-        if grp == 0:
-            first_step(grp, h_in)
-
-            @pl.loop(1, LAG)
-            def _(step):
-                head_step(grp, h_in, step, (grp, step - 1), None)
-        else:
-            head_step(grp, h_in, 0, (grp - 1, steps - 1), (grp - 1, steps - LAG))
-
-            @pl.loop(1, LAG)
-            def _(step):
-                head_step(grp, h_in, step, (grp, step - 1), (grp - 1, steps - LAG + step))
-
-        if grp + 1 < groups:
-            finish(1, grp + 1)
-
-        @pl.loop(LAG, steps)
-        def _(step):
-            head_step(grp, h_in, step, (grp, step - 1), (grp, step - LAG))
-
-    last = groups - 1
-    own_step(last, steps - 1)
+                if step + AHEAD < steps:
+                    head_copy(0, step + AHEAD).wait()
+        if entry >= LAG:
+            kl_wait(entry - LAG)
+        with scope(f"entry{entry}"):
+            z = jnp.concatenate([turned_dot(h_in, wh.at[step], row) for row in range(0, CHUNK, TILE)], axis=1)
+            zsend[step, rows] = scaled(z, 0, step)
+            if entry == 0:
+                z_copy(entry).start()
+            zkeep[step, rows] = scaled(dot_t(h_in, wh[step, CHUNK:2 * CHUNK]), 1, step)
+            if entry == step and step + AHEAD < steps:
+                turn_head(step + AHEAD)
+            if entry > 0:
+                own_step(entry - 1)
+            if entry >= LAG:
+                kl_step(entry - LAG)
+        if entry > 0:
+            z_copy(entry).start()
+
+    b_wait(1, 0)
+    h_in = normed_rows(1, 0, SIZES[0])
+    for entry in range(steps):
+        if entry == LATE:
+            finish(1, 1)
+        head_entry(entry, h_in)
+    b_wait(1, 1)
+    h_in = normed_rows(1, SIZES[0], SIZES[1])
+    for entry in range(steps, 2 * steps):
+        head_entry(entry, h_in)
+
+    own_step(len(entries) - 1)
 
     def to_row(col):
         return jnp.sum(jnp.where(eye, col, 0.0), axis=0, keepdims=True)
@@ -377,9 +411,9 @@
             d_copy(red, grp).wait_send()
             y_copy(red, grp).wait_send()
             b_copy(red, grp).wait_send()
-    for step in range(steps - LAG, steps):
-        kl_wait(last, step)
-        kl_step(last, step)
+    for entry in range(len(entries) - LAG, len(entries)):
+        kl_wait(entry)
+        kl_step(entry)
     pack[here, 2:3, 0:tokens], pack[here, 3:4, 0:tokens] = stat_rows(m_kl, s_kl)
 
     def p_copy(hop):
@@ -390,10 +424,8 @@
 
     for hop in range(1, 8):
         p_copy(hop).start()
-    for grp in range(groups):
-        @pl.loop(0, steps)
-        def _(step):
-            z_copy(grp, step).wait_send()
+    for entry in range(len(entries)):
+        z_copy(entry).wait_send()
 
     with scope("wait_p"):
         for hop in range(1, 8):
@@ -450,8 +482,7 @@
                 pltpu.VMEM(b_value.shape, BF16),
                 pltpu.VMEM((q_rows + 2 * wide, dim), BF16),
                 pltpu.VMEM((2, q_rows, cols), BF16),
-                pltpu.VMEM((ff, dim), BF16),
-                pltpu.VMEM((ff, dim), BF16),
+                pltpu.VMEM((2 * ff, dim), BF16),
                 pltpu.VMEM((2, ff, cols), BF16),
                 pltpu.VMEM((steps, 2 * CHUNK, dim), BF16),
                 pltpu.VMEM((2, tokens, cols), F32),
@@ -461,6 +492,7 @@
                 pltpu.VMEM((2, tokens, cols), F32),
                 pltpu.VMEM((2, tokens, cols), F32),
                 pltpu.VMEM((2, 2, tokens, cols), F32),
+                pltpu.VMEM((tokens, 2 * ff), F32),
                 pltpu.VMEM((steps, tokens, CHUNK), F32),
                 pltpu.VMEM((steps, tokens, CHUNK), F32),
                 pltpu.VMEM((steps, tokens, CHUNK), F32),
@@ -473,7 +505,7 @@
                 pltpu.VMEM((8, 8, 128), F32),
                 sem((22,)), sem((2, steps)),
                 sem((2, groups)), sem((2, groups)), sem((2, groups)), sem((2, groups)), sem((2, groups)), sem((2, groups)),
-                sem((groups, steps)), sem((groups, steps)), sem((7,)), sem((7,)),
+                sem((groups * steps,)), sem((groups * steps,)), sem((7,)), sem((7,)),
             ],
             compiler_params=pltpu.CompilerParams(
                 collective_id=0, has_side_effects=True, vmem_limit_bytes=67043328),

time: 58.3 us -> 55.8 us (0.957)
  Pallas kernels: 56.3 us -> 53.8 us
    pallas_call x1, Pallas kernels: 56.3 us -> 53.8 us  [per_device(): pl.pallas_call(functools.partial(kernel, (tokens, dim, head_dim, q_heads,...]
where the time goes in v3:
time: 55.8 us; the launch traced here: 55.7 us
  Pallas kernels  53.8 us (96%)
  local copies, waits for them, and re-layouts  1.25 us (2%)
  between operations  0.65 us (1%)
    pallas_call x1, Pallas kernels, per_device(): pl.pallas_call(functools.partial(kernel, (tokens, dim, head_dim, q_heads,...  53.8 us
    squeeze x1, local copies, waits for them, and re-layouts, per_device(): return (out[0], out[1])  1.25 us

profile of v3, /device:TPU:0, one launch (start us, length us, event | category | flops | bytes accessed | tf_op | source)
XLA Modules:
  0.0 55.7 jit_solution(3075849183467359360)
XLA Ops:
  0.6 53.8 %layer_head_kl.1 = f32[2,64]{1,0:T(2,128)} custom-call(bf16[2,64,2048]{2,1,0:T(8,128)(2,1)} %hidden.1, f32[3,2,2048]{2,1,0:T(2,128)} %bitcast.8, bf16[512,2048]{1,0:T(8,128)(2,1)} %w_query.1, bf16[128,2048]{1,0:T(8,128)(2,1)} %w_key.1, bf16[128,2048]{1,0:T(8,128)(2,1)} %w_value.1, bf16[512,2048]{1,0:T(8,128)(2,1)} %w_out.1, bf16[1408,2048]{1,0:T(8,128)(2,1)} %w_gate.1, ...), custom_call_target="tpu_custom_call" | custom-call | tf_op jit(solution)/shard_map/layer_head_kl/pallas_call | solution.py:469
  54.4 1.3 %slice_bitcast_fusion = (f32[64]{0:T(128)}, f32[64]{0:T(128)}) fusion(f32[2,64]{1,0:T(2,128)} %layer_head_kl.1), kind=kLoop, calls=%fused_computation | loop fusion | bytes 1024 | tf_op jit(solution)/shard_map/squeeze | solution.py:515

commit v4 on v3

--- a/solution.py
+++ b/solution.py
@@ -15,6 +15,7 @@
 NEG = -1e30
 SIZES = (24, 40)
 AHEAD = 4
+SPARE = 2
 LATE = 6
 TILE = 256
 CHUNK = 512
@@ -44,7 +45,7 @@
 def kernel(cfg, hidden, gains, w_query, w_key, w_value, w_out, w_gate, w_up, w_down, w_head,
            seg_in, mask_in, tgt_in, bq_in, bk_in, bv_in, out_ref,
            xb, gn, seg_ref, mask_ref, tgt_ref, bq_ref, bk_ref, bv_ref, wqkv, wo, wgu, wd, wh, xcol, qs, os_, part, rbuf, ybuf, full,
-           gate_up, zsend, zkeep, zrecv, m_own, s_own, m_kl, s_kl, t_acc, dup, pack,
+           gate_up, zsend, zkeep, zrecv, m_own, s_own, m_kl, s_kl, t_acc, dup, pack, pack_kl,
            in_sem, head_sem, d_send, d_recv, y_send, y_recv, b_send, b_recv, z_send, z_recv, p_send, p_recv):
     tokens, dim, head_dim, q_heads, vocab = cfg
     offs = [sum(SIZES[:grp]) for grp in range(len(SIZES))]
@@ -72,12 +73,12 @@
     moves = [(hidden.at[half], xb), (gains, gn), (seg_in, seg_ref), (mask_in, mask_ref), (tgt_in, tgt_ref),
              (bq_in, bq_ref), (bk_in, bk_ref), (bv_in, bv_ref)]
     n_small = len(moves)
-    for piece in range(4):
-        rows = pl.ds(piece * q_rows // 4, q_rows // 4)
-        moves.append((w_query.at[rows], wqkv.at[rows]))
     for slot in range(2):
-        moves.append((w_key.at[kv_rows], wqkv.at[pl.ds(q_rows + slot * head_dim, head_dim)]))
-        moves.append((w_value.at[kv_rows], wqkv.at[pl.ds(q_rows + (2 + slot) * head_dim, head_dim)]))
+        moves.append((w_key.at[kv_rows], wqkv.at[pl.ds(slot * head_dim, head_dim)]))
+        moves.append((w_value.at[kv_rows], wqkv.at[pl.ds((2 + slot) * head_dim, head_dim)]))
+    for piece in range(2):
+        moves.append((w_query.at[pl.ds(piece * q_rows // 2, q_rows // 2)],
+                      wqkv.at[pl.ds(2 * wide + piece * q_rows // 2, q_rows // 2)]))
     n_qkv = len(moves)
     moves += [(w_out.at[:, theirs_cols], wo.at[0]), (w_out.at[:, mine_cols], wo.at[1])]
     n_out = len(moves)
@@ -147,8 +148,8 @@
         turned = jnp.where(low, pltpu.roll(vals, wide - half_dim, 1), pltpu.roll(vals, half_dim, 1))
         return vals * cos_t + turned * sin_t
 
-    with scope("wait_qkv"):
-        for copy in loads[n_small:n_qkv]:
+    with scope("wait_kv"):
+        for copy in loads[n_small:n_small + 5]:
             copy.wait()
     for copy in loads[n_qkv:]:
         copy.start()
@@ -158,15 +159,23 @@
         head_copy(0, step).start()
         head_copy(1, step).start()
 
-    with scope("qkv"):
-        qkv = dot_t(a_in, wqkv[...])
-        k_rot = rotate(qkv[:, q_rows:q_rows + wide] + bias_k).astype(BF16)
-        v_two = (qkv[:, q_rows + wide:q_rows + 2 * wide] + bias_v).astype(BF16)
-        for pair in range(q_heads // 2):
+    def put_q(first_pair, vals):
+        for idx in range(q_heads // 4):
+            pair = first_pair + idx
             bias_q = jnp.where(even, bias[2 * pair:2 * pair + 1], bias[2 * pair + 1:2 * pair + 2])
-            q_rot = rotate(qkv[:, pair * wide:(pair + 1) * wide] + bias_q) * head_dim ** -0.5
+            q_rot = rotate(vals[:, idx * wide:(idx + 1) * wide] + bias_q) * head_dim ** -0.5
             qs[2 * pair * tokens:(2 * pair + 1) * tokens, :] = jnp.where(even, q_rot, 0.0).astype(BF16)
             qs[(2 * pair + 1) * tokens:(2 * pair + 2) * tokens, :] = jnp.where(even, 0.0, q_rot).astype(BF16)
+
+    cut = 2 * wide + q_rows // 2
+    with scope("qkv"):
+        kvq = dot_t(a_in, wqkv[0:cut])
+        loads[n_small + 5].wait()
+        rest = dot_t(a_in, wqkv[cut:cut + q_rows // 2])
+        k_rot = rotate(kvq[:, :wide] + bias_k).astype(BF16)
+        v_two = (kvq[:, wide:2 * wide] + bias_v).astype(BF16)
+        put_q(0, kvq[:, 2 * wide:])
+        put_q(q_heads // 4, rest)
     with scope("attn"):
         scores = dot_t(qs[...], k_rot).reshape(q_heads, tokens, tokens)
         scores = jnp.where(allowed[None], scores, NEG)
@@ -183,17 +192,17 @@
 
     def d_copy(red, grp):
         return pltpu.make_async_remote_copy(
-            part.at[red, 0, rows_of(grp)], rbuf.at[red, rows_of(grp)], d_send.at[red, grp], d_recv.at[red, grp],
+            part.at[red, 0, rows_of(grp)], rbuf.at[red, rows_of(grp)], d_send, d_recv.at[red, grp],
             device_id=d_peer, device_id_type=MESH)
 
     def y_copy(red, grp):
         return pltpu.make_async_remote_copy(
-            part.at[red, 1, rows_of(grp)], ybuf.at[red, rows_of(grp)], y_send.at[red, grp], y_recv.at[red, grp],
+            part.at[red, 1, rows_of(grp)], ybuf.at[red, rows_of(grp)], y_send, y_recv.at[red, grp],
             device_id=y_peer, device_id_type=MESH)
 
     def b_copy(red, grp):
         return pltpu.make_async_remote_copy(
-            full.at[red, core, rows_of(grp)], full.at[red, core, rows_of(grp)], b_send.at[red, grp], b_recv.at[red, grp],
+            full.at[red, core, rows_of(grp)], full.at[red, core, rows_of(grp)], b_send, b_recv.at[red, grp],
             device_id=d_peer, device_id_type=MESH)
 
     def chip_sum(red, grp):
@@ -284,8 +293,9 @@
     loads[n_out].wait()
     turn(0, early)
     loads[n_out + 1].wait()
-    turn(early, blocks)
+    turn(early, blocks - SPARE)
     finish(0, 0)
+    turn(blocks - SPARE, blocks)
     for grp in range(groups):
         mlp(grp, gathered(0, grp))
         if grp + 1 < groups:
@@ -310,7 +320,7 @@
         step, off, size = entries[entry]
         rows = pl.ds(off, size)
         return pltpu.make_async_remote_copy(
-            zsend.at[step, rows], zrecv.at[step, rows], z_send.at[entry], z_recv.at[entry],
+            zsend.at[step, rows], zrecv.at[step, rows], z_send, z_recv.at[entry],
             device_id=x_peer, device_id_type=MESH)
 
     def scaled(z, keep, step):
@@ -404,32 +414,37 @@
         s_col = jnp.sum(s_ref[...] * jnp.exp(m_all - m_col), axis=1, keepdims=True)
         return to_row(m_col), to_row(s_col)
 
+    packs = (pack, pack_kl)
+
+    def p_copy(which, hop):
+        other = (here + hop) % 8
+        return pltpu.make_async_remote_copy(
+            packs[which].at[here], packs[which].at[here], p_send.at[which], p_recv.at[which],
+            device_id={"tp": other % 2, "role": other // 2}, device_id_type=MESH)
+
+    def p_all(which):
+        seven = packs[which].at[pl.ds(0, 7)]
+        return pltpu.make_async_remote_copy(
+            seven, seven, p_send.at[which], p_recv.at[which], device_id=x_peer, device_id_type=MESH)
+
     pack[here, 0:1, 0:tokens], pack[here, 1:2, 0:tokens] = stat_rows(m_own, s_own)
-    pack[here, 4:5, 0:tokens] = to_row(jnp.sum(t_acc[...], axis=1, keepdims=True))
-    for red in range(2):
-        for grp in range(groups):
-            d_copy(red, grp).wait_send()
-            y_copy(red, grp).wait_send()
-            b_copy(red, grp).wait_send()
+    pack[here, 2:3, 0:tokens] = to_row(jnp.sum(t_acc[...], axis=1, keepdims=True))
+    for hop in range(1, 8):
+        p_copy(0, hop).start()
+    for send in (d_send, y_send, b_send):
+        pltpu.make_async_remote_copy(rbuf, rbuf, send, d_recv.at[0, 0], device_id=d_peer, device_id_type=MESH).wait_send()
     for entry in range(len(entries) - LAG, len(entries)):
         kl_wait(entry)
         kl_step(entry)
-    pack[here, 2:3, 0:tokens], pack[here, 3:4, 0:tokens] = stat_rows(m_kl, s_kl)
-
-    def p_copy(hop):
-        other = (here + hop) % 8
-        return pltpu.make_async_remote_copy(
-            pack.at[here], pack.at[here], p_send.at[hop - 1], p_recv.at[hop - 1],
-            device_id={"tp": other % 2, "role": other // 2}, device_id_type=MESH)
-
+    pack_kl[here, 0:1, 0:tokens], pack_kl[here, 1:2, 0:tokens] = stat_rows(m_kl, s_kl)
     for hop in range(1, 8):
-        p_copy(hop).start()
-    for entry in range(len(entries)):
-        z_copy(entry).wait_send()
-
+        p_copy(1, hop).start()
+    pltpu.make_async_remote_copy(zsend, zsend, z_send, z_recv.at[0], device_id=x_peer, device_id_type=MESH).wait_send()
+    p_all(0).wait_send()
+    with scope("wait_p0"):
+        p_all(0).wait_recv()
     with scope("wait_p"):
-        for hop in range(1, 8):
-            p_copy(hop).wait_recv()
+        p_all(1).wait_recv()
 
     with scope("final"):
         def lse(devices):
@@ -440,14 +455,12 @@
 
         lse_pol = lse(range(4))
         lse_ref = lse(range(4, 8))
-        cross = functools.reduce(jnp.add, [pack[dev, 3:4, 0:tokens] * jnp.exp(pack[dev, 2:3, 0:tokens] - lse_pol) for dev in range(8)])
-        tgt_z = functools.reduce(jnp.add, [pack[dev, 4:5, 0:tokens] for dev in range(4)])
+        cross = functools.reduce(jnp.add, [pack_kl[dev, 1:2, 0:tokens] * jnp.exp(pack_kl[dev, 0:1, 0:tokens] - lse_pol) for dev in range(8)])
+        tgt_z = functools.reduce(jnp.add, [pack[dev, 2:3, 0:tokens] for dev in range(4)])
         mask_vals = mask_ref[...].astype(F32)
         out_ref[0:1, :] = (cross - lse_pol + lse_ref) * mask_vals
         out_ref[1:2, :] = (tgt_z - lse_pol) * mask_vals
-    with scope("wait_ps"):
-        for hop in range(1, 8):
-            p_copy(hop).wait_send()
+    p_all(1).wait_send()
 
 
 def solution(mesh):
@@ -468,7 +481,7 @@
         sem = pltpu.SemaphoreType.DMA
         out = pl.pallas_call(
             functools.partial(kernel, (tokens, dim, head_dim, q_heads, vocab)),
-            out_shape=jax.ShapeDtypeStruct((2, tokens), F32),
+            out_shape=pltpu.VMEM((2, tokens), F32),
             in_specs=[pl.BlockSpec(memory_space=pl.ANY)] * 16,
             out_specs=pl.BlockSpec(memory_space=pltpu.VMEM),
             scratch_shapes=[
@@ -502,13 +515,14 @@
                 pltpu.VMEM((tokens, 128), F32),
                 pltpu.VMEM((tokens, 128), F32),
                 pltpu.VMEM((16, 128), F32),
-                pltpu.VMEM((8, 8, 128), F32),
-                sem((22,)), sem((2, steps)),
-                sem((2, groups)), sem((2, groups)), sem((2, groups)), sem((2, groups)), sem((2, groups)), sem((2, groups)),
-                sem((groups * steps,)), sem((groups * steps,)), sem((7,)), sem((7,)),
+                pltpu.VMEM((8, 4, 128), F32),
+                pltpu.VMEM((8, 2, 128), F32),
+                sem((20,)), sem((2, steps)),
+                sem(()), sem((2, groups)), sem(()), sem((2, groups)), sem(()), sem((2, groups)),
+                sem(()), sem((groups * steps,)), sem((2,)), sem((2,)),
             ],
             compiler_params=pltpu.CompilerParams(
-                collective_id=0, has_side_effects=True, vmem_limit_bytes=67043328),
+                collective_id=0, has_side_effects=True, vmem_limit_bytes=64500000),
             name="layer_head_kl",
         )(hidden, jnp.transpose(norm_gains, (1, 0, 2)), w_query, w_key, w_value, w_out, w_gate, w_up, w_down, w_head,
           segment_ids.reshape(1, tokens), loss_mask.reshape(1, tokens), target.reshape(1, tokens), b_query, b_key, b_value)

time: 55.8 us -> 53.9 us (0.966)
  Pallas kernels: 53.8 us -> 52.7 us
  local copies, waits for them, and re-layouts: 1.25 us -> 0.52 us
    pallas_call x1, Pallas kernels: 53.8 us -> 52.7 us  [per_device(): pl.pallas_call(functools.partial(kernel, (tokens, dim, head_dim, q_heads,...]
    squeeze x1, local copies, waits for them, and re-layouts: 1.25 us -> 0.52 us  [per_device(): return (out[0], out[1])]
where the time goes in v4:
time: 53.9 us; the launch traced here: 53.8 us
  Pallas kernels  52.7 us (98%)
  between operations  0.65 us (1%)
    pallas_call x1, Pallas kernels, per_device(): pl.pallas_call(functools.partial(kernel, (tokens, dim, head_dim, q_heads,...  52.7 us

profile of v4, /device:TPU:0, one launch (start us, length us, event | category | flops | bytes accessed | tf_op | source)
XLA Modules:
  0.0 53.8 jit_solution(12652346790992834808)
XLA Ops:
  0.6 52.7 %layer_head_kl.1 = f32[2,64]{1,0:T(2,128)S(1)} custom-call(bf16[2,64,2048]{2,1,0:T(8,128)(2,1)} %hidden.1, f32[3,2,2048]{2,1,0:T(2,128)} %bitcast.8, bf16[512,2048]{1,0:T(8,128)(2,1)} %w_query.1, bf16[128,2048]{1,0:T(8,128)(2,1)} %w_key.1, bf16[128,2048]{1,0:T(8,128)(2,1)} %w_value.1, bf16[512,2048]{1,0:T(8,128)(2,1)} %w_out.1, bf16[1408,2048]{1,0:T(8,128)(2,1)} %w_gate.1, ...), custom_call_target="tpu_custom_call" | custom-call | tf_op jit(solution)/shard_map/layer_head_kl/pallas_call | solution.py:482
  53.3 0.5 slice_bitcast_fusion

commit v5 on v4

--- a/solution.py
+++ b/solution.py
@@ -16,10 +16,8 @@
 SIZES = (24, 40)
 AHEAD = 4
 SPARE = 2
-LATE = 6
 TILE = 256
 CHUNK = 512
-LAG = 5
 F32 = jnp.float32
 BF16 = jnp.bfloat16
 MESH = pl.DeviceIdType.MESH
@@ -85,7 +83,9 @@
     moves += [(w_gate, wgu.at[pl.ds(0, ff)]), (w_up, wgu.at[pl.ds(ff, ff)])]
     n_gu = len(moves)
     moves += [(w_down.at[:, theirs_cols], wd.at[0]), (w_down.at[:, mine_cols], wd.at[1])]
-    loads = [pltpu.make_async_copy(src, dst, in_sem.at[idx]) for idx, (src, dst) in enumerate(moves)]
+    bounds = [n_small, n_small + 5, n_qkv, n_out, n_out + 1, n_gu]
+    loads = [pltpu.make_async_copy(src, dst, in_sem.at[sum(idx >= bound for bound in bounds)])
+             for idx, (src, dst) in enumerate(moves)]
     for copy in loads[:n_qkv]:
         copy.start()
 
@@ -102,7 +102,7 @@
     def head_copy(keep, step):
         start, _ = chunk_start((1 - send_half) if keep else send_half, step)
         return pltpu.make_async_copy(w_head.at[pl.ds(pl.multiple_of(start, 64), CHUNK)],
-                                     wh.at[step, pl.ds(keep * CHUNK, CHUNK)], head_sem.at[keep, step])
+                                     wh.at[step, pl.ds(keep * CHUNK, CHUNK)], head_sem.at[step])
 
     ti = lax.broadcasted_iota(jnp.int32, (tokens, tokens), 0)
     tj = lax.broadcasted_iota(jnp.int32, (tokens, tokens), 1)
@@ -263,6 +263,7 @@
         if grp == groups - 1:
             for step in range(AHEAD):
                 head_copy(0, step).wait()
+                head_copy(1, step).wait()
         with scope(f"mlp{grp}"):
             if grp == groups - 1:
                 for step in range(AHEAD):
@@ -314,96 +315,73 @@
     def split(vals):
         return [vals[:, 128 * t:128 * (t + 1)] for t in range(tiles)]
 
-    entries = [(step, offs[grp], SIZES[grp]) for grp in range(groups) for step in range(steps)]
-
-    def z_copy(entry):
-        step, off, size = entries[entry]
-        rows = pl.ds(off, size)
+    everyone = pl.ds(0, tokens)
+
+    def z_copy(grp, step):
         return pltpu.make_async_remote_copy(
-            zsend.at[step, rows], zrecv.at[step, rows], z_send, z_recv.at[entry],
+            zsend.at[step, rows_of(grp)], zrecv.at[step, rows_of(grp)], z_send, z_recv.at[(1 + step) if grp else 0],
             device_id=x_peer, device_id_type=MESH)
 
     def scaled(z, keep, step):
         _, repeated = chunk_start((1 - send_half) if keep else send_half, step)
         return jnp.where(lanes >= repeated, z * (1.0 / TEMPERATURE), NEG)
 
-    def own_step(entry):
-        step, off, size = entries[entry]
-        rows = pl.ds(off, size)
-        m_old, total, hits = m_own[rows], s_own[rows], t_acc[rows]
-        goal = tgt_col[off:off + size]
+    def own_step(step):
+        m_old, total, hits = m_own[...], s_own[...], t_acc[...]
         parts = []
         for keep, src in ((0, zsend), (1, zkeep)):
             start, repeated = chunk_start((1 - send_half) if keep else send_half, step)
-            z = src[step, rows]
+            z = src[step]
             ids = (lanes + (shard * vocab + start)).astype(F32)
-            for hit in split(jnp.where((ids == goal) & (lanes >= repeated), z, 0.0)):
+            for hit in split(jnp.where((ids == tgt_col) & (lanes >= repeated), z, 0.0)):
                 hits = hits + hit
             parts += split(z)
         m_new = functools.reduce(jnp.maximum, parts, m_old)
         total = total * jnp.exp(m_old - m_new)
         for piece in parts:
             total = total + jnp.exp(piece - m_new)
-        m_own[rows] = m_new
-        s_own[rows] = total
-        t_acc[rows] = hits
-
-    def kl_wait(entry):
-        with scope(f"wait_z{entry}"):
-            z_copy(entry).wait_recv()
-
-    def kl_step(entry):
-        step, off, size = entries[entry]
-        rows = pl.ds(off, size)
-        mine, theirs = zkeep[step, rows], zrecv[step, rows]
+        m_own[...] = m_new
+        s_own[...] = total
+        t_acc[...] = hits
+
+    def kl_step(step):
+        with scope(f"wait_z{step}"):
+            z_copy(groups - 1, step).wait_recv()
+        mine, theirs = zkeep[step], zrecv[step]
         policy = half == 0
         tops = split(jnp.where(policy, mine, theirs))
         diffs = split(jnp.where(policy, mine - theirs, theirs - mine))
-        m_old = m_kl[rows]
+        m_old = m_kl[...]
         m_new = functools.reduce(jnp.maximum, tops, m_old)
-        total = s_kl[rows] * jnp.exp(m_old - m_new)
+        total = s_kl[...] * jnp.exp(m_old - m_new)
         for top, diff in zip(tops, diffs):
             total = total + jnp.exp(top - m_new) * diff
-        m_kl[rows] = m_new
-        s_kl[rows] = total
-
-    def head_entry(entry, h_in):
-        step, off, size = entries[entry]
-        rows = pl.ds(off, size)
-        if entry == step:
-            with scope("wait_w"):
-                head_copy(1, step).wait()
-                if step + AHEAD < steps:
+        m_kl[...] = m_new
+        s_kl[...] = total
+
+    for grp in range(groups):
+        h_in = gathered(1, grp)
+        for step in range(steps):
+            if grp == 0 and step + AHEAD < steps:
+                with scope("wait_w"):
                     head_copy(0, step + AHEAD).wait()
-        if entry >= LAG:
-            kl_wait(entry - LAG)
-        with scope(f"entry{entry}"):
-            z = jnp.concatenate([turned_dot(h_in, wh.at[step], row) for row in range(0, CHUNK, TILE)], axis=1)
-            zsend[step, rows] = scaled(z, 0, step)
-            if entry == 0:
-                z_copy(entry).start()
-            zkeep[step, rows] = scaled(dot_t(h_in, wh[step, CHUNK:2 * CHUNK]), 1, step)
-            if entry == step and step + AHEAD < steps:
-                turn_head(step + AHEAD)
-            if entry > 0:
-                own_step(entry - 1)
-            if entry >= LAG:
-                kl_step(entry - LAG)
-        if entry > 0:
-            z_copy(entry).start()
-
-    b_wait(1, 0)
-    h_in = normed_rows(1, 0, SIZES[0])
-    for entry in range(steps):
-        if entry == LATE:
-            finish(1, 1)
-        head_entry(entry, h_in)
-    b_wait(1, 1)
-    h_in = normed_rows(1, SIZES[0], SIZES[1])
-    for entry in range(steps, 2 * steps):
-        head_entry(entry, h_in)
-
-    own_step(len(entries) - 1)
+                    head_copy(1, step + AHEAD).wait()
+            with scope(f"send{grp}"):
+                z = jnp.concatenate([turned_dot(h_in, wh.at[step], row) for row in range(0, CHUNK, TILE)], axis=1)
+                zsend[step, rows_of(grp)] = scaled(z, 0, step)
+                if grp == 0 and step + AHEAD < steps:
+                    turn_head(step + AHEAD)
+            z_copy(grp, step).start()
+        if grp + 1 < groups:
+            finish(1, grp + 1)
+    h_in = normed_rows(1, 0, tokens)
+    for step in range(steps):
+        with scope("keep"):
+            zkeep[step] = scaled(dot_t(h_in, wh[step, CHUNK:2 * CHUNK]), 1, step)
+            if step > 0:
+                own_step(step - 1)
+    own_step(steps - 1)
+
 
     def to_row(col):
         return jnp.sum(jnp.where(eye, col, 0.0), axis=0, keepdims=True)
@@ -433,9 +411,10 @@
         p_copy(0, hop).start()
     for send in (d_send, y_send, b_send):
         pltpu.make_async_remote_copy(rbuf, rbuf, send, d_recv.at[0, 0], device_id=d_peer, device_id_type=MESH).wait_send()
-    for entry in range(len(entries) - LAG, len(entries)):
-        kl_wait(entry)
-        kl_step(entry)
+    early = zrecv.at[pl.ds(0, steps), rows_of(0)]
+    pltpu.make_async_remote_copy(early, early, z_send, z_recv.at[0], device_id=x_peer, device_id_type=MESH).wait_recv()
+    for step in range(steps):
+        kl_step(step)
     pack_kl[here, 0:1, 0:tokens], pack_kl[here, 1:2, 0:tokens] = stat_rows(m_kl, s_kl)
     for hop in range(1, 8):
         p_copy(1, hop).start()
@@ -517,9 +496,9 @@
                 pltpu.VMEM((16, 128), F32),
                 pltpu.VMEM((8, 4, 128), F32),
                 pltpu.VMEM((8, 2, 128), F32),
-                sem((20,)), sem((2, steps)),
+                sem((7,)), sem((steps,)),
                 sem(()), sem((2, groups)), sem(()), sem((2, groups)), sem(()), sem((2, groups)),
-                sem(()), sem((groups * steps,)), sem((2,)), sem((2,)),
+                sem(()), sem((1 + steps,)), sem((2,)), sem((2,)),
             ],
             compiler_params=pltpu.CompilerParams(
                 collective_id=0, has_side_effects=True, vmem_limit_bytes=64500000),

time: 53.9 us -> 52.4 us (0.972)
  Pallas kernels: 52.7 us -> 51.2 us
    pallas_call x1, Pallas kernels: 52.7 us -> 51.2 us  [per_device(): pl.pallas_call(functools.partial(kernel, (tokens, dim, head_dim, q_heads,...]
where the time goes in v5:
time: 52.4 us; the launch traced here: 52.3 us
  Pallas kernels  51.2 us (98%)
  between operations  0.65 us (1%)
    pallas_call x1, Pallas kernels, per_device(): pl.pallas_call(functools.partial(kernel, (tokens, dim, head_dim, q_heads,...  51.2 us

profile of v5, /device:TPU:0, one launch (start us, length us, event | category | flops | bytes accessed | tf_op | source)
XLA Modules:
  0.0 52.3 jit_solution(16075603798614622547)
XLA Ops:
  0.6 51.2 %layer_head_kl.1 = f32[2,64]{1,0:T(2,128)S(1)} custom-call(bf16[2,64,2048]{2,1,0:T(8,128)(2,1)} %hidden.1, f32[3,2,2048]{2,1,0:T(2,128)} %bitcast.8, bf16[512,2048]{1,0:T(8,128)(2,1)} %w_query.1, bf16[128,2048]{1,0:T(8,128)(2,1)} %w_key.1, bf16[128,2048]{1,0:T(8,128)(2,1)} %w_value.1, bf16[512,2048]{1,0:T(8,128)(2,1)} %w_out.1, bf16[1408,2048]{1,0:T(8,128)(2,1)} %w_gate.1, ...), custom_call_target="tpu_custom_call" | custom-call | tf_op jit(solution)/shard_map/layer_head_kl/pallas_call | solution.py:461
  51.8 0.5 slice_bitcast_fusion

commit v6 on v5

--- a/solution.py
+++ b/solution.py
@@ -15,6 +15,7 @@
 NEG = -1e30
 SIZES = (24, 40)
 AHEAD = 4
+DIRECT = 256
 SPARE = 2
 TILE = 256
 CHUNK = 512
@@ -42,9 +43,9 @@
 
 def kernel(cfg, hidden, gains, w_query, w_key, w_value, w_out, w_gate, w_up, w_down, w_head,
            seg_in, mask_in, tgt_in, bq_in, bk_in, bv_in, out_ref,
-           xb, gn, seg_ref, mask_ref, tgt_ref, bq_ref, bk_ref, bv_ref, wqkv, wo, wgu, wd, wh, xcol, qs, os_, part, rbuf, ybuf, full,
+           xb, gn, seg_ref, mask_ref, tgt_ref, bq_ref, bk_ref, bv_ref, wqkv, wo, wgu, wd, wh, xcol, qs, os_, part, rbuf, ybuf, dbuf, full,
            gate_up, zsend, zkeep, zrecv, m_own, s_own, m_kl, s_kl, t_acc, dup, pack, pack_kl,
-           in_sem, head_sem, d_send, d_recv, y_send, y_recv, b_send, b_recv, z_send, z_recv, p_send, p_recv):
+           in_sem, head_sem, d_send, d_recv, y_send, y_recv, c_send, c_recv, b_send, b_recv, z_send, z_recv, p_send, p_recv):
     tokens, dim, head_dim, q_heads, vocab = cfg
     offs = [sum(SIZES[:grp]) for grp in range(len(SIZES))]
     groups = len(SIZES)
@@ -60,6 +61,7 @@
     shard = core * 2 + tp
     d_peer = {"role": half * 2 + 1 - core}
     y_peer = {"tp": 1 - tp}
+    c_peer = {"tp": 1 - tp, "role": half * 2 + 1 - core}
     x_peer = {"role": (1 - half) * 2 + core}
     send_half = 1 - half
     q_rows = q_heads * head_dim
@@ -195,10 +197,19 @@
             part.at[red, 0, rows_of(grp)], rbuf.at[red, rows_of(grp)], d_send, d_recv.at[red, grp],
             device_id=d_peer, device_id_type=MESH)
 
+    def summed(grp):
+        return pl.ds(DIRECT, cols - DIRECT) if grp == 0 else pl.ds(0, cols)
+
     def y_copy(red, grp):
-        return pltpu.make_async_remote_copy(
-            part.at[red, 1, rows_of(grp)], ybuf.at[red, rows_of(grp)], y_send, y_recv.at[red, grp],
+        place = (red, rows_of(grp), summed(grp))
+        return pltpu.make_async_remote_copy(
+            rbuf.at[place], ybuf.at[place], y_send.at[grp], y_recv.at[red, grp],
             device_id=y_peer, device_id_type=MESH)
+
+    def c_copy(red, mine):
+        return pltpu.make_async_remote_copy(
+            part.at[red, mine, rows_of(0), pl.ds(0, DIRECT)], dbuf.at[red, 1 - mine], c_send, c_recv.at[red],
+            device_id=y_peer if mine else c_peer, device_id_type=MESH)
 
     def b_copy(red, grp):
         return pltpu.make_async_remote_copy(
@@ -209,15 +220,21 @@
         rows = rows_of(grp)
         with scope(f"wait_d{red}{grp}"):
             d_copy(red, grp).wait_recv()
-        part[red, 1, rows] = part[red, 1, rows] + rbuf[red, rows]
+        rbuf[red, rows] = part[red, 1, rows] + rbuf[red, rows]
         y_copy(red, grp).start()
 
     def finish(red, grp):
         rows = rows_of(grp)
         with scope(f"wait_y{red}{grp}"):
             y_copy(red, grp).wait_recv()
-        base = xcol[core, rows] if red == 0 else full[0, core, rows]
-        full[red, core, rows] = (base + (part[red, 1, rows] + ybuf[red, rows])).astype(BF16).astype(F32)
+        base = xcol if red == 0 else full.at[0]
+        place = (rows, summed(grp))
+        full[(red, core) + place] = (base[(core,) + place] + (rbuf[(red,) + place] + ybuf[(red,) + place])).astype(BF16).astype(F32)
+        if grp == 0:
+            pltpu.make_async_remote_copy(dbuf.at[red], dbuf.at[red], c_send, c_recv.at[red],
+                                         device_id=y_peer, device_id_type=MESH).wait_recv()
+            place = (rows, pl.ds(0, DIRECT))
+            full[(red, core) + place] = (base[(core,) + place] + (rbuf[(red,) + place] + (dbuf[red, 0] + dbuf[red, 1]))).astype(BF16).astype(F32)
         b_copy(red, grp).start()
 
     def b_wait(red, grp):
@@ -274,8 +291,16 @@
             act = (gate * (1.0 / (1.0 + jnp.exp(-gate))) * up).astype(BF16)
             part[1, 0, rows] = dot_n(act, wd[0])
         d_copy(1, grp).start()
+        if grp == 0:
+            c_copy(1, 0).start()
+        if grp + 1 < groups:
+            finish(0, grp + 1)
+        else:
+            finish(1, 0)
         with scope(f"down{grp}"):
             part[1, 1, rows] = dot_n(act, wd[1])
+        if grp == 0:
+            c_copy(1, 1).start()
 
     for copy in loads[n_qkv:n_out]:
         copy.wait()
@@ -283,10 +308,13 @@
         part[0, 0] = dot_n(os_[...], wo[0])
     with scope("entry"):
         pl.semaphore_wait(barrier, 7)
-    for grp in range(groups):
+    d_copy(0, 0).start()
+    c_copy(0, 0).start()
+    for grp in range(1, groups):
         d_copy(0, grp).start()
     with scope("oproj"):
         part[0, 1] = dot_n(os_[...], wo[1])
+    c_copy(0, 1).start()
     blocks = 2 * ff // TILE
     early = ff // TILE
     for grp in range(groups):
@@ -299,10 +327,6 @@
     turn(blocks - SPARE, blocks)
     for grp in range(groups):
         mlp(grp, gathered(0, grp))
-        if grp + 1 < groups:
-            finish(0, grp + 1)
-        if grp == groups - 1:
-            finish(1, 0)
         chip_sum(1, grp)
 
     for stat in (s_own, s_kl, t_acc):
@@ -317,9 +341,10 @@
 
     everyone = pl.ds(0, tokens)
 
-    def z_copy(grp, step):
-        return pltpu.make_async_remote_copy(
-            zsend.at[step, rows_of(grp)], zrecv.at[step, rows_of(grp)], z_send, z_recv.at[(1 + step) if grp else 0],
+    def z_copy(grp, step, lanes_of=pl.ds(0, CHUNK)):
+        place = (step, rows_of(grp), lanes_of)
+        return pltpu.make_async_remote_copy(
+            zsend.at[place], zrecv.at[place], z_send, z_recv.at[(1 + step) if grp else 0],
             device_id=x_peer, device_id_type=MESH)
 
     def scaled(z, keep, step):
@@ -362,15 +387,24 @@
     for grp in range(groups):
         h_in = gathered(1, grp)
         for step in range(steps):
-            if grp == 0 and step + AHEAD < steps:
+            late = step + AHEAD - 1 if grp == 0 and 0 < step <= steps - AHEAD else None
+            if late is not None:
                 with scope("wait_w"):
-                    head_copy(0, step + AHEAD).wait()
-                    head_copy(1, step + AHEAD).wait()
+                    head_copy(0, late).wait()
+                    head_copy(1, late).wait()
+            rows = range(0, CHUNK, TILE)
+            if grp == 0 and step == 0:
+                for row in rows:
+                    place = pl.ds(row, TILE)
+                    with scope("first"):
+                        zsend[step, rows_of(grp), place] = turned_dot(h_in, wh.at[step], row) * (1.0 / TEMPERATURE)
+                    z_copy(grp, step, place).start()
+                continue
             with scope(f"send{grp}"):
-                z = jnp.concatenate([turned_dot(h_in, wh.at[step], row) for row in range(0, CHUNK, TILE)], axis=1)
+                z = jnp.concatenate([turned_dot(h_in, wh.at[step], row) for row in rows], axis=1)
                 zsend[step, rows_of(grp)] = scaled(z, 0, step)
-                if grp == 0 and step + AHEAD < steps:
-                    turn_head(step + AHEAD)
+                if late is not None:
+                    turn_head(late)
             z_copy(grp, step).start()
         if grp + 1 < groups:
             finish(1, grp + 1)
@@ -409,8 +443,10 @@
     pack[here, 2:3, 0:tokens] = to_row(jnp.sum(t_acc[...], axis=1, keepdims=True))
     for hop in range(1, 8):
         p_copy(0, hop).start()
-    for send in (d_send, y_send, b_send):
-        pltpu.make_async_remote_copy(rbuf, rbuf, send, d_recv.at[0, 0], device_id=d_peer, device_id_type=MESH).wait_send()
+    sent = [(rbuf, d_send), (rbuf, b_send), (dbuf, c_send)]
+    sent += [(rbuf.at[pl.ds(0, 2), rows_of(grp), summed(grp)], y_send.at[grp]) for grp in range(groups)]
+    for ref, send in sent:
+        pltpu.make_async_remote_copy(ref, ref, send, c_recv.at[0], device_id=d_peer, device_id_type=MESH).wait_send()
     early = zrecv.at[pl.ds(0, steps), rows_of(0)]
     pltpu.make_async_remote_copy(early, early, z_send, z_recv.at[0], device_id=x_peer, device_id_type=MESH).wait_recv()
     for step in range(steps):
@@ -483,6 +519,7 @@
                 pltpu.VMEM((2, 2, tokens, cols), F32),
                 pltpu.VMEM((2, tokens, cols), F32),
                 pltpu.VMEM((2, tokens, cols), F32),
+                pltpu.VMEM((2, 2, SIZES[0], DIRECT), F32),
                 pltpu.VMEM((2, 2, tokens, cols), F32),
                 pltpu.VMEM((tokens, 2 * ff), F32),
                 pltpu.VMEM((steps, tokens, CHUNK), F32),
@@ -497,7 +534,7 @@
                 pltpu.VMEM((8, 4, 128), F32),
                 pltpu.VMEM((8, 2, 128), F32),
                 sem((7,)), sem((steps,)),
-                sem(()), sem((2, groups)), sem(()), sem((2, groups)), sem(()), sem((2, groups)),
+                sem(()), sem((2, groups)), sem((groups,)), sem((2, groups)), sem(()), sem((2,)), sem(()), sem((2, groups)),
                 sem(()), sem((1 + steps,)), sem((2,)), sem((2,)),
             ],
             compiler_params=pltpu.CompilerParams(

time: 52.4 us -> 51.4 us (0.981)
  Pallas kernels: 51.2 us -> 50.1 us
    pallas_call x1, Pallas kernels: 51.2 us -> 50.1 us  [per_device(): pl.pallas_call(functools.partial(kernel, (tokens, dim, head_dim, q_heads,...]
where the time goes in v6:
time: 51.4 us; the launch traced here: 51.3 us
  Pallas kernels  50.1 us (97%)
  between operations  0.65 us (1%)
  local copies, waits for them, and re-layouts  0.52 us (1%)
    pallas_call x1, Pallas kernels, per_device(): pl.pallas_call(functools.partial(kernel, (tokens, dim, head_dim, q_heads,...  50.1 us

profile of v6, /device:TPU:0, one launch (start us, length us, event | category | flops | bytes accessed | tf_op | source)
XLA Modules:
  0.0 51.3 jit_solution(6512035701286507569)
XLA Ops:
  0.6 50.1 %layer_head_kl.1 = f32[2,64]{1,0:T(2,128)S(1)} custom-call(bf16[2,64,2048]{2,1,0:T(8,128)(2,1)} %hidden.1, f32[3,2,2048]{2,1,0:T(2,128)} %bitcast.8, bf16[512,2048]{1,0:T(8,128)(2,1)} %w_query.1, bf16[128,2048]{1,0:T(8,128)(2,1)} %w_key.1, bf16[128,2048]{1,0:T(8,128)(2,1)} %w_value.1, bf16[512,2048]{1,0:T(8,128)(2,1)} %w_out.1, bf16[1408,2048]{1,0:T(8,128)(2,1)} %w_gate.1, ...), custom_call_target="tpu_custom_call" | custom-call | tf_op jit(solution)/shard_map/layer_head_kl/pallas_call | solution.py:497
  50.7 0.5 %slice_bitcast_fusion = (f32[64]{0:T(128)}, f32[64]{0:T(128)}) fusion(f32[2,64]{1,0:T(2,128)S(1)} %layer_head_kl.1), kind=kLoop, calls=%fused_computation | loop fusion | bytes 1024 | tf_op jit(solution)/shard_map/squeeze | solution.py:545

commit v7 on v6

--- a/solution.py
+++ b/solution.py
@@ -17,6 +17,7 @@
 AHEAD = 4
 DIRECT = 256
 SPARE = 2
+SOON = 3
 TILE = 256
 CHUNK = 512
 F32 = jnp.float32
@@ -43,7 +44,7 @@
 
 def kernel(cfg, hidden, gains, w_query, w_key, w_value, w_out, w_gate, w_up, w_down, w_head,
            seg_in, mask_in, tgt_in, bq_in, bk_in, bv_in, out_ref,
-           xb, gn, seg_ref, mask_ref, tgt_ref, bq_ref, bk_ref, bv_ref, wqkv, wo, wgu, wd, wh, xcol, qs, os_, part, rbuf, ybuf, dbuf, full,
+           xb, gn, seg_ref, mask_ref, tgt_ref, bq_ref, bk_ref, bv_ref, wqkv, wo, wgu, wd, wh, xcol, qs, part, rbuf, ybuf, dbuf, full,
            gate_up, zsend, zkeep, zrecv, m_own, s_own, m_kl, s_kl, t_acc, dup, pack, pack_kl,
            in_sem, head_sem, d_send, d_recv, y_send, y_recv, c_send, c_recv, b_send, b_recv, z_send, z_recv, p_send, p_recv):
     tokens, dim, head_dim, q_heads, vocab = cfg
@@ -70,25 +71,28 @@
     kv_rows = pl.ds(pl.multiple_of(tp * head_dim, head_dim), head_dim)
     theirs_cols = pl.ds(pl.multiple_of((1 - core) * cols, cols), cols)
     mine_cols = pl.ds(pl.multiple_of(core * cols, cols), cols)
+    kv_two = 2 * head_dim
     moves = [(hidden.at[half], xb), (gains, gn), (seg_in, seg_ref), (mask_in, mask_ref), (tgt_in, tgt_ref),
              (bq_in, bq_ref), (bk_in, bk_ref), (bv_in, bv_ref)]
     n_small = len(moves)
-    for slot in range(2):
-        moves.append((w_key.at[kv_rows], wqkv.at[pl.ds(slot * head_dim, head_dim)]))
-        moves.append((w_value.at[kv_rows], wqkv.at[pl.ds((2 + slot) * head_dim, head_dim)]))
-    for piece in range(2):
-        moves.append((w_query.at[pl.ds(piece * q_rows // 2, q_rows // 2)],
-                      wqkv.at[pl.ds(2 * wide + piece * q_rows // 2, q_rows // 2)]))
+    moves += [(w_key.at[kv_rows], wqkv.at[pl.ds(0, head_dim)]), (w_value.at[kv_rows], wqkv.at[pl.ds(head_dim, head_dim)])]
+    n_first = []
+    cuts = (0, TILE, 2 * TILE, kv_two + q_rows)
+    for begin, end in zip(cuts, cuts[1:]):
+        low_row = max(begin - kv_two, 0)
+        moves.append((w_query.at[pl.ds(low_row, end - kv_two - low_row)],
+                      wqkv.at[pl.ds(kv_two + low_row, end - kv_two - low_row)]))
+        n_first.append(len(moves))
     n_qkv = len(moves)
     moves += [(w_out.at[:, theirs_cols], wo.at[0]), (w_out.at[:, mine_cols], wo.at[1])]
     n_out = len(moves)
     moves += [(w_gate, wgu.at[pl.ds(0, ff)]), (w_up, wgu.at[pl.ds(ff, ff)])]
     n_gu = len(moves)
     moves += [(w_down.at[:, theirs_cols], wd.at[0]), (w_down.at[:, mine_cols], wd.at[1])]
-    bounds = [n_small, n_small + 5, n_qkv, n_out, n_out + 1, n_gu]
+    bounds = [n_small] + n_first + [n_out, n_out + 1, n_gu]
     loads = [pltpu.make_async_copy(src, dst, in_sem.at[sum(idx >= bound for bound in bounds)])
              for idx, (src, dst) in enumerate(moves)]
-    for copy in loads[:n_qkv]:
+    for copy in loads[:n_out]:
         copy.start()
 
     barrier = pltpu.get_barrier_semaphore()
@@ -150,10 +154,20 @@
         turned = jnp.where(low, pltpu.roll(vals, wide - half_dim, 1), pltpu.roll(vals, half_dim, 1))
         return vals * cos_t + turned * sin_t
 
+    def q_store(pair, vals):
+        bias_q = jnp.where(even, bias[2 * pair:2 * pair + 1], bias[2 * pair + 1:2 * pair + 2])
+        q_rot = rotate(vals + bias_q) * head_dim ** -0.5
+        for odd in range(2):
+            head = jnp.where(even, 0.0, q_rot) if odd else jnp.where(even, q_rot, 0.0)
+            for grp in range(groups):
+                off, size = offs[grp], SIZES[grp]
+                start = q_heads * off + (2 * pair + odd) * size
+                qs[start:start + size, :] = head[off:off + size].astype(BF16)
+
     with scope("wait_kv"):
-        for copy in loads[n_small:n_small + 5]:
+        for copy in loads[n_small:n_first[0]]:
             copy.wait()
-    for copy in loads[n_qkv:]:
+    for copy in loads[n_out:]:
         copy.start()
 
     @pl.loop(0, steps)
@@ -161,33 +175,36 @@
         head_copy(0, step).start()
         head_copy(1, step).start()
 
-    def put_q(first_pair, vals):
-        for idx in range(q_heads // 4):
-            pair = first_pair + idx
-            bias_q = jnp.where(even, bias[2 * pair:2 * pair + 1], bias[2 * pair + 1:2 * pair + 2])
-            q_rot = rotate(vals[:, idx * wide:(idx + 1) * wide] + bias_q) * head_dim ** -0.5
-            qs[2 * pair * tokens:(2 * pair + 1) * tokens, :] = jnp.where(even, q_rot, 0.0).astype(BF16)
-            qs[(2 * pair + 1) * tokens:(2 * pair + 2) * tokens, :] = jnp.where(even, 0.0, q_rot).astype(BF16)
-
-    cut = 2 * wide + q_rows // 2
     with scope("qkv"):
-        kvq = dot_t(a_in, wqkv[0:cut])
-        loads[n_small + 5].wait()
-        rest = dot_t(a_in, wqkv[cut:cut + q_rows // 2])
-        k_rot = rotate(kvq[:, :wide] + bias_k).astype(BF16)
-        v_two = (kvq[:, wide:2 * wide] + bias_v).astype(BF16)
-        put_q(0, kvq[:, 2 * wide:])
-        put_q(q_heads // 4, rest)
-    with scope("attn"):
-        scores = dot_t(qs[...], k_rot).reshape(q_heads, tokens, tokens)
-        scores = jnp.where(allowed[None], scores, NEG)
+        dots = [dot_t(a_in, wqkv[cuts[0]:cuts[1]])]
+        for copy in loads[n_first[0]:n_first[1]]:
+            copy.wait()
+        dots.append(dot_t(a_in, wqkv[cuts[1]:cuts[2]]))
+        kv = dots[0][:, :wide]
+        other = pltpu.roll(kv, head_dim, 1)
+        k_rot = rotate(jnp.where(even, kv, other) + bias_k).astype(BF16)
+        v_two = (jnp.where(even, other, kv) + bias_v).astype(BF16)
+        q_store(0, dots[0][:, wide:2 * wide])
+        for copy in loads[n_first[1]:n_first[2]]:
+            copy.wait()
+        dots.append(dot_t(a_in, wqkv[cuts[2]:cuts[3]]))
+        q_store(1, dots[1][:, :wide])
+        q_store(2, dots[1][:, wide:])
+        q_store(3, dots[2])
+    def attend(grp):
+        off, size = offs[grp], SIZES[grp]
+        keys = off + size
+        scores = dot_t(qs[q_heads * off:q_heads * keys], k_rot[:keys]).reshape(q_heads, size, keys)
+        scores = jnp.where(allowed[None, off:keys, :keys], scores, NEG)
         expd = jnp.exp(scores - jnp.max(scores, axis=-1, keepdims=True))
-        probs = (expd / jnp.sum(expd, axis=-1, keepdims=True)).astype(BF16).reshape(q_heads * tokens, tokens)
-        heads_out = dot_n(probs, v_two)
+        probs = (expd / jnp.sum(expd, axis=-1, keepdims=True)).astype(BF16).reshape(q_heads * size, keys)
+        heads_out = dot_n(probs, v_two[:keys])
+        outs = []
         for pair in range(q_heads // 2):
-            lo = heads_out[2 * pair * tokens:(2 * pair + 1) * tokens]
-            hi = heads_out[(2 * pair + 1) * tokens:(2 * pair + 2) * tokens]
-            os_[:, pair * wide:(pair + 1) * wide] = jnp.where(even, lo, hi).astype(BF16)
+            lo = heads_out[2 * pair * size:(2 * pair + 1) * size]
+            hi = heads_out[(2 * pair + 1) * size:(2 * pair + 2) * size]
+            outs.append(jnp.where(even, lo, hi).astype(BF16))
+        return jnp.concatenate(outs, axis=1)
 
     def rows_of(grp):
         return pl.ds(offs[grp], SIZES[grp])
@@ -302,25 +319,32 @@
         if grp == 0:
             c_copy(1, 1).start()
 
-    for copy in loads[n_qkv:n_out]:
-        copy.wait()
-    with scope("oproj"):
-        part[0, 0] = dot_n(os_[...], wo[0])
-    with scope("entry"):
-        pl.semaphore_wait(barrier, 7)
-    d_copy(0, 0).start()
-    c_copy(0, 0).start()
-    for grp in range(1, groups):
+    for grp in range(groups):
+        with scope(f"attn{grp}"):
+            mixed = attend(grp)
+        if grp == 0:
+            for copy in loads[n_qkv:n_out]:
+                copy.wait()
+        if grp == 1:
+            chip_sum(0, 0)
+        with scope("oproj"):
+            part[0, 0, rows_of(grp)] = dot_n(mixed, wo[0])
+        if grp == 0:
+            with scope("entry"):
+                pl.semaphore_wait(barrier, 7)
         d_copy(0, grp).start()
-    with scope("oproj"):
-        part[0, 1] = dot_n(os_[...], wo[1])
-    c_copy(0, 1).start()
+        if grp == 0:
+            c_copy(0, 0).start()
+        with scope("oproj"):
+            part[0, 1, rows_of(grp)] = dot_n(mixed, wo[1])
+        if grp == 0:
+            c_copy(0, 1).start()
     blocks = 2 * ff // TILE
     early = ff // TILE
-    for grp in range(groups):
-        chip_sum(0, grp)
     loads[n_out].wait()
-    turn(0, early)
+    turn(0, SOON)
+    chip_sum(0, 1)
+    turn(SOON, early)
     loads[n_out + 1].wait()
     turn(early, blocks - SPARE)
     finish(0, 0)
@@ -508,14 +532,13 @@
                 pltpu.VMEM(b_query.shape, BF16),
                 pltpu.VMEM(b_key.shape, BF16),
                 pltpu.VMEM(b_value.shape, BF16),
-                pltpu.VMEM((q_rows + 2 * wide, dim), BF16),
+                pltpu.VMEM((q_rows + wide, dim), BF16),
                 pltpu.VMEM((2, q_rows, cols), BF16),
                 pltpu.VMEM((2 * ff, dim), BF16),
                 pltpu.VMEM((2, ff, cols), BF16),
                 pltpu.VMEM((steps, 2 * CHUNK, dim), BF16),
                 pltpu.VMEM((2, tokens, cols), F32),
                 pltpu.VMEM((q_heads * tokens, wide), BF16),
-                pltpu.VMEM((tokens, q_rows), BF16),
                 pltpu.VMEM((2, 2, tokens, cols), F32),
                 pltpu.VMEM((2, tokens, cols), F32),
                 pltpu.VMEM((2, tokens, cols), F32),
@@ -533,7 +556,7 @@
                 pltpu.VMEM((16, 128), F32),
                 pltpu.VMEM((8, 4, 128), F32),
                 pltpu.VMEM((8, 2, 128), F32),
-                sem((7,)), sem((steps,)),
+                sem((8,)), sem((steps,)),
                 sem(()), sem((2, groups)), sem((groups,)), sem((2, groups)), sem(()), sem((2,)), sem(()), sem((2, groups)),
                 sem(()), sem((1 + steps,)), sem((2,)), sem((2,)),
             ],

time: 51.4 us -> 51.1 us (level)
  no operation moved by 1% of the time
where the time goes in v7:
time: 51.1 us; the launch traced here: 51 us
  Pallas kernels  49.9 us (98%)
  between operations  0.65 us (1%)
  local copies, waits for them, and re-layouts  0.52 us (1%)
    pallas_call x1, Pallas kernels, per_device(): pl.pallas_call(functools.partial(kernel, (tokens, dim, head_dim, q_heads,...  49.9 us

profile of v7, /device:TPU:0, one launch (start us, length us, event | category | flops | bytes accessed | tf_op | source)
XLA Modules:
  0.0 51.0 jit_solution(12156532766459097340)
XLA Ops:
  0.6 49.9 %layer_head_kl.1 = f32[2,64]{1,0:T(2,128)S(1)} custom-call(bf16[2,64,2048]{2,1,0:T(8,128)(2,1)} %hidden.1, f32[3,2,2048]{2,1,0:T(2,128)} %bitcast.8, bf16[512,2048]{1,0:T(8,128)(2,1)} %w_query.1, bf16[128,2048]{1,0:T(8,128)(2,1)} %w_key.1, bf16[128,2048]{1,0:T(8,128)(2,1)} %w_value.1, bf16[512,2048]{1,0:T(8,128)(2,1)} %w_out.1, bf16[1408,2048]{1,0:T(8,128)(2,1)} %w_gate.1, ...), custom_call_target="tpu_custom_call" | custom-call | tf_op jit(solution)/shard_map/layer_head_kl/pallas_call | solution.py:521
  50.5 0.5 %slice_bitcast_fusion = (f32[64]{0:T(128)}, f32[64]{0:T(128)}) fusion(f32[2,64]{1,0:T(2,128)S(1)} %layer_head_kl.1), kind=kLoop, calls=%fused_computation | loop fusion | bytes 1024 | tf_op jit(solution)/shard_map/squeeze | solution.py:568

commit v8 on v7

--- a/solution.py
+++ b/solution.py
@@ -13,11 +13,13 @@
 ROPE_BASE = 1000000.0
 TEMPERATURE = 0.7
 NEG = -1e30
-SIZES = (24, 40)
+SIZES = (16, 48)
+LATER = ((0, 16), (16, 24), (40, 24))
 AHEAD = 4
-DIRECT = 256
+DIRECT = 384
 SPARE = 2
-SOON = 3
+SOON = 2
+FINISH = (7, 5)
 TILE = 256
 CHUNK = 512
 F32 = jnp.float32
@@ -206,21 +208,24 @@
             outs.append(jnp.where(even, lo, hi).astype(BF16))
         return jnp.concatenate(outs, axis=1)
 
-    def rows_of(grp):
-        return pl.ds(offs[grp], SIZES[grp])
+    ranges = (tuple(zip(offs, SIZES)), LATER)
+    later_of = ((0,), (1, 2))
+
+    def rows_of(grp, red=0):
+        return pl.ds(*ranges[red][grp])
 
     def d_copy(red, grp):
         return pltpu.make_async_remote_copy(
-            part.at[red, 0, rows_of(grp)], rbuf.at[red, rows_of(grp)], d_send, d_recv.at[red, grp],
+            part.at[red, 0, rows_of(grp, red)], rbuf.at[red, rows_of(grp, red)], d_send, d_recv.at[red, grp],
             device_id=d_peer, device_id_type=MESH)
 
     def summed(grp):
         return pl.ds(DIRECT, cols - DIRECT) if grp == 0 else pl.ds(0, cols)
 
     def y_copy(red, grp):
-        place = (red, rows_of(grp), summed(grp))
-        return pltpu.make_async_remote_copy(
-            rbuf.at[place], ybuf.at[place], y_send.at[grp], y_recv.at[red, grp],
+        place = (red, rows_of(grp, red), summed(grp))
+        return pltpu.make_async_remote_copy(
+            rbuf.at[place], ybuf.at[place], y_send.at[min(grp, 1)], y_recv.at[red, grp],
             device_id=y_peer, device_id_type=MESH)
 
     def c_copy(red, mine):
@@ -230,18 +235,18 @@
 
     def b_copy(red, grp):
         return pltpu.make_async_remote_copy(
-            full.at[red, core, rows_of(grp)], full.at[red, core, rows_of(grp)], b_send, b_recv.at[red, grp],
+            full.at[red, core, rows_of(grp, red)], full.at[red, core, rows_of(grp, red)], b_send, b_recv.at[red, grp],
             device_id=d_peer, device_id_type=MESH)
 
     def chip_sum(red, grp):
-        rows = rows_of(grp)
+        rows = rows_of(grp, red)
         with scope(f"wait_d{red}{grp}"):
             d_copy(red, grp).wait_recv()
         rbuf[red, rows] = part[red, 1, rows] + rbuf[red, rows]
         y_copy(red, grp).start()
 
     def finish(red, grp):
-        rows = rows_of(grp)
+        rows = rows_of(grp, red)
         with scope(f"wait_y{red}{grp}"):
             y_copy(red, grp).wait_recv()
         base = xcol if red == 0 else full.at[0]
@@ -269,17 +274,16 @@
 
     def gathered(red, grp):
         b_wait(red, grp)
-        return normed_rows(red, offs[grp], SIZES[grp])
+        return normed_rows(red, *ranges[red][grp])
 
     def turn_tiles(ref, rows):
         for k in range(dim // TILE):
             ref[rows, k * TILE:(k + 1) * TILE] = ref[rows, k * TILE:(k + 1) * TILE].T
 
-    def turn(first, last):
+    def turn(first, end):
         with scope("turn"):
-            @pl.loop(first, last)
-            def _(blk):
-                turn_tiles(wgu, pl.ds(pl.multiple_of(blk * TILE, TILE), TILE))
+            for blk in range(first, end):
+                turn_tiles(wgu, pl.ds(blk * TILE, TILE))
 
     def turn_head(step):
         for row in range(0, CHUNK, TILE):
@@ -307,7 +311,8 @@
             gate, up = gate_up[rows, 0:ff], gate_up[rows, ff:2 * ff]
             act = (gate * (1.0 / (1.0 + jnp.exp(-gate))) * up).astype(BF16)
             part[1, 0, rows] = dot_n(act, wd[0])
-        d_copy(1, grp).start()
+        for late in later_of[grp]:
+            d_copy(1, late).start()
         if grp == 0:
             c_copy(1, 0).start()
         if grp + 1 < groups:
@@ -351,7 +356,8 @@
     turn(blocks - SPARE, blocks)
     for grp in range(groups):
         mlp(grp, gathered(0, grp))
-        chip_sum(1, grp)
+        for late in later_of[grp]:
+            chip_sum(1, late)
 
     for stat in (s_own, s_kl, t_acc):
         stat[...] = jnp.zeros_like(stat)
@@ -363,12 +369,12 @@
     def split(vals):
         return [vals[:, 128 * t:128 * (t + 1)] for t in range(tiles)]
 
-    everyone = pl.ds(0, tokens)
+    last = len(LATER) - 1
 
     def z_copy(grp, step, lanes_of=pl.ds(0, CHUNK)):
-        place = (step, rows_of(grp), lanes_of)
-        return pltpu.make_async_remote_copy(
-            zsend.at[place], zrecv.at[place], z_send, z_recv.at[(1 + step) if grp else 0],
+        place = (step, rows_of(grp, 1), lanes_of)
+        return pltpu.make_async_remote_copy(
+            zsend.at[place], zrecv.at[place], z_send, z_recv.at[grp + (step if grp == last else 0)],
             device_id=x_peer, device_id_type=MESH)
 
     def scaled(z, keep, step):
@@ -395,7 +401,7 @@
 
     def kl_step(step):
         with scope(f"wait_z{step}"):
-            z_copy(groups - 1, step).wait_recv()
+            z_copy(last, step).wait_recv()
         mine, theirs = zkeep[step], zrecv[step]
         policy = half == 0
         tops = split(jnp.where(policy, mine, theirs))
@@ -408,9 +414,11 @@
         m_kl[...] = m_new
         s_kl[...] = total
 
-    for grp in range(groups):
+    for grp in range(last + 1):
         h_in = gathered(1, grp)
         for step in range(steps):
+            if grp < last and step == FINISH[grp]:
+                finish(1, grp + 1)
             late = step + AHEAD - 1 if grp == 0 and 0 < step <= steps - AHEAD else None
             if late is not None:
                 with scope("wait_w"):
@@ -421,17 +429,15 @@
                 for row in rows:
                     place = pl.ds(row, TILE)
                     with scope("first"):
-                        zsend[step, rows_of(grp), place] = turned_dot(h_in, wh.at[step], row) * (1.0 / TEMPERATURE)
+                        zsend[step, rows_of(grp, 1), place] = turned_dot(h_in, wh.at[step], row) * (1.0 / TEMPERATURE)
                     z_copy(grp, step, place).start()
                 continue
             with scope(f"send{grp}"):
                 z = jnp.concatenate([turned_dot(h_in, wh.at[step], row) for row in rows], axis=1)
-                zsend[step, rows_of(grp)] = scaled(z, 0, step)
+                zsend[step, rows_of(grp, 1)] = scaled(z, 0, step)
                 if late is not None:
                     turn_head(late)
             z_copy(grp, step).start()
-        if grp + 1 < groups:
-            finish(1, grp + 1)
     h_in = normed_rows(1, 0, tokens)
     for step in range(steps):
         with scope("keep"):
@@ -471,8 +477,9 @@
     sent += [(rbuf.at[pl.ds(0, 2), rows_of(grp), summed(grp)], y_send.at[grp]) for grp in range(groups)]
     for ref, send in sent:
         pltpu.make_async_remote_copy(ref, ref, send, c_recv.at[0], device_id=d_peer, device_id_type=MESH).wait_send()
-    early = zrecv.at[pl.ds(0, steps), rows_of(0)]
-    pltpu.make_async_remote_copy(early, early, z_send, z_recv.at[0], device_id=x_peer, device_id_type=MESH).wait_recv()
+    for grp in range(last):
+        whole = zrecv.at[pl.ds(0, steps), rows_of(grp, 1)]
+        pltpu.make_async_remote_copy(whole, whole, z_send, z_recv.at[grp], device_id=x_peer, device_id_type=MESH).wait_recv()
     for step in range(steps):
         kl_step(step)
     pack_kl[here, 0:1, 0:tokens], pack_kl[here, 1:2, 0:tokens] = stat_rows(m_kl, s_kl)
@@ -557,8 +564,8 @@
                 pltpu.VMEM((8, 4, 128), F32),
                 pltpu.VMEM((8, 2, 128), F32),
                 sem((8,)), sem((steps,)),
-                sem(()), sem((2, groups)), sem((groups,)), sem((2, groups)), sem(()), sem((2,)), sem(()), sem((2, groups)),
-                sem(()), sem((1 + steps,)), sem((2,)), sem((2,)),
+                sem(()), sem((2, 3)), sem((groups,)), sem((2, 3)), sem(()), sem((2,)), sem(()), sem((2, 3)),
+                sem(()), sem((2 + steps,)), sem((2,)), sem((2,)),
             ],
             compiler_params=pltpu.CompilerParams(
                 collective_id=0, has_side_effects=True, vmem_limit_bytes=64500000),

time: 51.1 us -> 50.3 us (0.984)
  Pallas kernels: 49.9 us -> 49.1 us
    pallas_call x1, Pallas kernels: 49.9 us -> 49.1 us  [per_device(): pl.pallas_call(functools.partial(kernel, (tokens, dim, head_dim, q_heads,...]
where the time goes in v8:
time: 50.3 us; the launch traced here: 50.2 us
  Pallas kernels  49.1 us (98%)
  between operations  0.65 us (1%)
  local copies, waits for them, and re-layouts  0.52 us (1%)
    pallas_call x1, Pallas kernels, per_device(): pl.pallas_call(functools.partial(kernel, (tokens, dim, head_dim, q_heads,...  49.1 us

profile of v8, /device:TPU:0, one launch (start us, length us, event | category | flops | bytes accessed | tf_op | source)
XLA Modules:
  0.0 50.2 jit_solution(12706389071332942102)
XLA Ops:
  0.6 49.1 %layer_head_kl.1 = f32[2,64]{1,0:T(2,128)S(1)} custom-call(bf16[2,64,2048]{2,1,0:T(8,128)(2,1)} %hidden.1, f32[3,2,2048]{2,1,0:T(2,128)} %bitcast.8, bf16[512,2048]{1,0:T(8,128)(2,1)} %w_query.1, bf16[128,2048]{1,0:T(8,128)(2,1)} %w_key.1, bf16[128,2048]{1,0:T(8,128)(2,1)} %w_value.1, bf16[512,2048]{1,0:T(8,128)(2,1)} %w_out.1, bf16[1408,2048]{1,0:T(8,128)(2,1)} %w_gate.1, ...), custom_call_target="tpu_custom_call" | custom-call | tf_op jit(solution)/shard_map/layer_head_kl/pallas_call | solution.py:528
  49.7 0.5 %slice_bitcast_fusion = (f32[64]{0:T(128)}, f32[64]{0:T(128)}) fusion(f32[2,64]{1,0:T(2,128)S(1)} %layer_head_kl.1), kind=kLoop, calls=%fused_computation | loop fusion | bytes 1024 | tf_op jit(solution)/shard_map/squeeze | solution.py:575

commit v9 on v8

--- a/solution.py
+++ b/solution.py
@@ -458,11 +458,15 @@
 
     packs = (pack, pack_kl)
 
+    flips = ((1, 0, 1), (1, 1, 1), (1, 0, 0), (1, 1, 0), (0, 0, 1), (0, 1, 1), (0, 1, 0))
+    pairs = ((tp, 1 - tp), (core, 1 - core), (half, 1 - half))
+
     def p_copy(which, hop):
-        other = (here + hop) % 8
+        to_half, to_core, to_tp = flips[hop - 1]
+        target = {"tp": pairs[0][to_tp], "role": pairs[2][to_half] * 2 + pairs[1][to_core]}
         return pltpu.make_async_remote_copy(
             packs[which].at[here], packs[which].at[here], p_send.at[which], p_recv.at[which],
-            device_id={"tp": other % 2, "role": other // 2}, device_id_type=MESH)
+            device_id=target, device_id_type=MESH)
 
     def p_all(which):
         seven = packs[which].at[pl.ds(0, 7)]

time: 50.3 us -> 50.3 us (level)
  no operation moved by 1% of the time
where the time goes in v9:
time: 50.3 us; the launch traced here: 50.2 us
  Pallas kernels  49 us (97%)
  between operations  0.65 us (1%)
  local copies, waits for them, and re-layouts  0.52 us (1%)
    pallas_call x1, Pallas kernels, per_device(): pl.pallas_call(functools.partial(kernel, (tokens, dim, head_dim, q_heads,...  49 us

profile of v9, /device:TPU:0, one launch (start us, length us, event | category | flops | bytes accessed | tf_op | source)
XLA Modules:
  0.0 50.2 jit_solution(4508241432861411317)
XLA Ops:
  0.6 49.0 %layer_head_kl.1 = f32[2,64]{1,0:T(2,128)S(1)} custom-call(bf16[2,64,2048]{2,1,0:T(8,128)(2,1)} %hidden.1, f32[3,2,2048]{2,1,0:T(2,128)} %bitcast.8, bf16[512,2048]{1,0:T(8,128)(2,1)} %w_query.1, bf16[128,2048]{1,0:T(8,128)(2,1)} %w_key.1, bf16[128,2048]{1,0:T(8,128)(2,1)} %w_value.1, bf16[512,2048]{1,0:T(8,128)(2,1)} %w_out.1, bf16[1408,2048]{1,0:T(8,128)(2,1)} %w_gate.1, ...), custom_call_target="tpu_custom_call" | custom-call | tf_op jit(solution)/shard_map/layer_head_kl/pallas_call | solution.py:532
  49.7 0.5 %slice_bitcast_fusion = (f32[64]{0:T(128)}, f32[64]{0:T(128)}) fusion(f32[2,64]{1,0:T(2,128)S(1)} %layer_head_kl.1), kind=kLoop, calls=%fused_computation | loop fusion | bytes 1024 | tf_op jit(solution)/shard_map/squeeze | solution.py:579
